TPU v7x, 64 devices: a 2x2x8 block of a 4x4x8 slice. The times are simulated.
64 devices in a mesh: dp: 4 (over x, y), ep: 16 (over z, core).
Axes of the slice: x: 2, y: 2, z: 8, core: 2. Of those that a mesh axis runs over, the one named last changes fastest.
The devices are a block of a 4x4x8 slice.
Arguments:
- tokens: bfloat16 [16384, 2048], P(('dp', 'ep')), parts along dimension 0
- expert_ids: int32 [16384, 8], P(('dp', 'ep')), parts along dimension 0
- gate_wts: float32 [16384, 8], P(('dp', 'ep')), parts along dimension 0
- slot_ids: int32 [16384, 8], P(('dp', 'ep')), parts along dimension 0
- w_gate: bfloat16 [64, 2048, 1024], P('ep')
- w_up: bfloat16 [64, 2048, 1024], P('ep')
- w_down: bfloat16 [64, 1024, 2048], P('ep')
Outputs:
- output: bfloat16 [16384, 2048], P(('dp', 'ep')), parts along dimension 0
There are 4 independent parts. A program takes and returns all parts, laid end to end along the dimension named above; an argument that names none is the same for every part.
All inputs are finite; a program needn't handle non-finite values.
Results may differ from a plain program's by a relative error of at most 0.001.
Values are sent between devices in bfloat16 or wider.
A program may use at most 768 MiB of HBM per device.

v0:
```python
import functools
import jax
import jax.numpy as jnp
from jax import lax
from jax.sharding import PartitionSpec as P

CAP_NUM = 3
CAP_DEN = 2


def local_share(token_block, src_shard, my_rank, w_gate, w_up, w_down, shard_cap):
    token_blk, ids_blk, gates_blk, slots_blk = token_block
    num_local = w_gate.shape[0]
    tok_dev = token_blk.shape[0]
    local_id = ids_blk - my_rank * num_local
    keep_mask = (slots_blk >= 0) & (local_id >= 0) & (local_id < num_local)
    flat_slot = jnp.where(keep_mask, local_id * shard_cap + slots_blk - src_shard * shard_cap, num_local * shard_cap).reshape(-1)
    tok_index = jnp.broadcast_to(jnp.arange(tok_dev, dtype=jnp.int32)[:, None], ids_blk.shape).reshape(-1)
    slot_token = jnp.full((num_local * shard_cap,), tok_dev, jnp.int32).at[flat_slot].set(tok_index, mode='drop')
    slot_gate = jnp.zeros((num_local * shard_cap,), jnp.float32).at[flat_slot].set(gates_blk.reshape(-1), mode='drop')
    dispatched = jnp.take(token_blk, slot_token, axis=0, mode='fill', fill_value=0).reshape(num_local, shard_cap, -1)
    h_gate = jnp.einsum('ecd,edf->ecf', dispatched, w_gate, preferred_element_type=jnp.float32)
    h_up = jnp.einsum('ecd,edf->ecf', dispatched, w_up, preferred_element_type=jnp.float32)
    hidden = (jax.nn.silu(h_gate) * h_up).astype(jnp.bfloat16)
    expert_out = jnp.einsum('ecf,efd->ecd', hidden, w_down, preferred_element_type=jnp.float32)
    weighted = (expert_out * slot_gate.reshape(num_local, shard_cap, 1)).reshape(num_local * shard_cap, -1)
    return jnp.zeros((tok_dev, token_blk.shape[1]), jnp.float32).at[slot_token].add(weighted, mode='drop')


def solution(mesh):
    group_size = mesh.shape['ep']
    next_perm = [(dev_num, (dev_num + 1) % group_size) for dev_num in range(group_size)]
    row_spec = P(('dp', 'ep'), None)
    expert_spec = P('ep', None, None)

    def per_device(tokens, expert_ids, gate_wts, slot_ids, w_gate, w_up, w_down):
        my_rank = lax.axis_index('ep')
        tok_dev, top_k = expert_ids.shape
        shard_cap = CAP_NUM * tok_dev * top_k // (CAP_DEN * w_gate.shape[0] * group_size)
        expert_share = functools.partial(local_share, my_rank=my_rank, w_gate=w_gate, w_up=w_up, w_down=w_down, shard_cap=shard_cap)
        own_block = (tokens, expert_ids, gate_wts, slot_ids)
        home_part = expert_share(own_block, my_rank)
        visitor = lax.ppermute(own_block, 'ep', next_perm)
        accum = expert_share(visitor, (my_rank - 1) % group_size)

        def pass_on(hop_num, loop_state):
            visitor, accum = loop_state
            visitor, accum = lax.ppermute((visitor, accum), 'ep', next_perm)
            return visitor, accum + expert_share(visitor, (my_rank - hop_num) % group_size)

        visitor, accum = lax.fori_loop(2, group_size, pass_on, (visitor, accum))
        accum = lax.ppermute(accum, 'ep', next_perm)
        return (accum + home_part).astype(jnp.bfloat16)

    return jax.shard_map(per_device, mesh=mesh, in_specs=(row_spec, row_spec, row_spec, row_spec, expert_spec, expert_spec, expert_spec), out_specs=row_spec, check_vma=False)
```

profile of v0, /device:TPU:21, one launch (start us, length us, event | category | flops | bytes accessed | tf_op | source)
XLA Modules:
  0.0 1102.9 jit_solution(178890269089377126)
XLA Ops:
  68.9 13.6 %broadcast_multiply_fusion.1 = f32[4,48,2048]{2,1,0:T(8,128)S(1)} fusion(f32[4,48]{1,0:T(4,128)S(1)} %mul.134, bf16[4,1024,2048]{2,1,0:T(8,128)(2,1)} %param.17, f32[4,48,1024]{2,1,0:T(8,128)S(1)} %fusion.27, bf16[4,48,2048]{2,1,0:T(8,128)(2,1)S(1)} %bitcast.46, bf16[4,2048,1024]{2,1,0:T(8,128)(2,1)} %param.16), kind=kOutput, calls=%fused_computation.32 | convolution fusion | flops 1612185600 | bytes 36700928 | tf_op jit(solution)/shard_map/ecf,efd->ecd/dot_general | solution.py:25
  86.9 984.8 %while.23 = (s32[]{:T(128)}, bf16[256,2048]{1,0:T(8,128)(2,1)}, s32[256,8]{0,1:T(8,128)S(1)}, f32[256,8]{1,0:T(8,128)}, s32[256,8]{0,1:T(8,128)S(1)}, /*index=5*...) while((s32[]{:T(128)}, bf16[256,2048]{1,0:T(8,128)(2,1)}, ...), condition=%wide.region_7.9_spmd, body=%wide.region_3.0_spmd.sunk | while | flops 2418307840 | bytes 90453192 | solution.py:51
  94.3 11.4 %collective-permute-done.2 = f32[256,8]{1,0:T(8,128)S(1)} collective-permute-done((f32[256,8]{1,0:T(8,128)}, f32[256,8]{1,0:T(8,128)S(1)}, u32[]{:S(2)}, u32[]{:S(2)}) %collective-permute-start.2) | collective-permute-done | bytes 8224 | tf_op jit(solution)/shard_map/while/body/eval_jaxpr/ppermute | solution.py:48
  137.6 15.1 %broadcast_multiply_fusion.3 = f32[4,48,2048]{2,1,0:T(8,128)} fusion(f32[4,48]{1,0:T(4,128)S(1)} %mul.190, bf16[4,1024,2048]{2,1,0:T(8,128)(2,1)} %get-tuple-element.393, f32[4,48,1024]{2,1,0:T(8,128)} %fusion.59, bf16[4,48,2048]{2,1,0:T(8,128)(2,1)S(1)} %bitcast.41, bf16[4,2048,1024]{2,1,0:T(8,128)(2,1)} %get-tuple-element.392), kind=kOutput, calls=%fused_computation.12.clone.1 | convolution fusion | flops 1612185600 | bytes 36700928 | tf_op jit(solution)/shard_map/while/body/eval_jaxpr/ecf,efd->ecd/dot_general | solution.py:25
  164.2 11.4 %collective-permute-done.2 = f32[256,8]{1,0:T(8,128)S(1)} collective-permute-done((f32[256,8]{1,0:T(8,128)}, f32[256,8]{1,0:T(8,128)S(1)}, u32[]{:S(2)}, u32[]{:S(2)}) %collective-permute-start.2) | collective-permute-done | bytes 8224 | tf_op jit(solution)/shard_map/while/body/eval_jaxpr/ppermute | solution.py:48
  207.6 15.1 %broadcast_multiply_fusion.3 = f32[4,48,2048]{2,1,0:T(8,128)} fusion(f32[4,48]{1,0:T(4,128)S(1)} %mul.190, bf16[4,1024,2048]{2,1,0:T(8,128)(2,1)} %get-tuple-element.393, f32[4,48,1024]{2,1,0:T(8,128)} %fusion.59, bf16[4,48,2048]{2,1,0:T(8,128)(2,1)S(1)} %bitcast.41, bf16[4,2048,1024]{2,1,0:T(8,128)(2,1)} %get-tuple-element.392), kind=kOutput, calls=%fused_computation.12.clone.1 | convolution fusion | flops 1612185600 | bytes 36700928 | tf_op jit(solution)/shard_map/while/body/eval_jaxpr/ecf,efd->ecd/dot_general | solution.py:25
  235.4 10.2 collective-permute-done.2
  266.9 9.8 fusion.59
  277.6 15.1 %broadcast_multiply_fusion.3 = f32[4,48,2048]{2,1,0:T(8,128)} fusion(f32[4,48]{1,0:T(4,128)S(1)} %mul.190, bf16[4,1024,2048]{2,1,0:T(8,128)(2,1)} %get-tuple-element.393, f32[4,48,1024]{2,1,0:T(8,128)} %fusion.59, bf16[4,48,2048]{2,1,0:T(8,128)(2,1)S(1)} %bitcast.41, bf16[4,2048,1024]{2,1,0:T(8,128)(2,1)} %get-tuple-element.392), kind=kOutput, calls=%fused_computation.12.clone.1 | convolution fusion | flops 1612185600 | bytes 36700928 | tf_op jit(solution)/shard_map/while/body/eval_jaxpr/ecf,efd->ecd/dot_general | solution.py:25
  305.5 11.3 %collective-permute-done.2 = f32[256,8]{1,0:T(8,128)S(1)} collective-permute-done((f32[256,8]{1,0:T(8,128)}, f32[256,8]{1,0:T(8,128)S(1)}, u32[]{:S(2)}, u32[]{:S(2)}) %collective-permute-start.2) | collective-permute-done | bytes 8224 | tf_op jit(solution)/shard_map/while/body/eval_jaxpr/ppermute | solution.py:48
  348.8 15.1 %broadcast_multiply_fusion.3 = f32[4,48,2048]{2,1,0:T(8,128)} fusion(f32[4,48]{1,0:T(4,128)S(1)} %mul.190, bf16[4,1024,2048]{2,1,0:T(8,128)(2,1)} %get-tuple-element.393, f32[4,48,1024]{2,1,0:T(8,128)} %fusion.59, bf16[4,48,2048]{2,1,0:T(8,128)(2,1)S(1)} %bitcast.41, bf16[4,2048,1024]{2,1,0:T(8,128)(2,1)} %get-tuple-element.392), kind=kOutput, calls=%fused_computation.12.clone.1 | convolution fusion | flops 1612185600 | bytes 36700928 | tf_op jit(solution)/shard_map/while/body/eval_jaxpr/ecf,efd->ecd/dot_general | solution.py:25
  375.5 11.3 %collective-permute-done.2 = f32[256,8]{1,0:T(8,128)S(1)} collective-permute-done((f32[256,8]{1,0:T(8,128)}, f32[256,8]{1,0:T(8,128)S(1)}, u32[]{:S(2)}, u32[]{:S(2)}) %collective-permute-start.2) | collective-permute-done | bytes 8224 | tf_op jit(solution)/shard_map/while/body/eval_jaxpr/ppermute | solution.py:48
  418.8 15.1 %broadcast_multiply_fusion.3 = f32[4,48,2048]{2,1,0:T(8,128)} fusion(f32[4,48]{1,0:T(4,128)S(1)} %mul.190, bf16[4,1024,2048]{2,1,0:T(8,128)(2,1)} %get-tuple-element.393, f32[4,48,1024]{2,1,0:T(8,128)} %fusion.59, bf16[4,48,2048]{2,1,0:T(8,128)(2,1)S(1)} %bitcast.41, bf16[4,2048,1024]{2,1,0:T(8,128)(2,1)} %get-tuple-element.392), kind=kOutput, calls=%fused_computation.12.clone.1 | convolution fusion | flops 1612185600 | bytes 36700928 | tf_op jit(solution)/shard_map/while/body/eval_jaxpr/ecf,efd->ecd/dot_general | solution.py:25
  445.5 11.3 %collective-permute-done.2 = f32[256,8]{1,0:T(8,128)S(1)} collective-permute-done((f32[256,8]{1,0:T(8,128)}, f32[256,8]{1,0:T(8,128)S(1)}, u32[]{:S(2)}, u32[]{:S(2)}) %collective-permute-start.2) | collective-permute-done | bytes 8224 | tf_op jit(solution)/shard_map/while/body/eval_jaxpr/ppermute | solution.py:48
  488.9 15.1 %broadcast_multiply_fusion.3 = f32[4,48,2048]{2,1,0:T(8,128)} fusion(f32[4,48]{1,0:T(4,128)S(1)} %mul.190, bf16[4,1024,2048]{2,1,0:T(8,128)(2,1)} %get-tuple-element.393, f32[4,48,1024]{2,1,0:T(8,128)} %fusion.59, bf16[4,48,2048]{2,1,0:T(8,128)(2,1)S(1)} %bitcast.41, bf16[4,2048,1024]{2,1,0:T(8,128)(2,1)} %get-tuple-element.392), kind=kOutput, calls=%fused_computation.12.clone.1 | convolution fusion | flops 1612185600 | bytes 36700928 | tf_op jit(solution)/shard_map/while/body/eval_jaxpr/ecf,efd->ecd/dot_general | solution.py:25
  515.6 11.3 %collective-permute-done.2 = f32[256,8]{1,0:T(8,128)S(1)} collective-permute-done((f32[256,8]{1,0:T(8,128)}, f32[256,8]{1,0:T(8,128)S(1)}, u32[]{:S(2)}, u32[]{:S(2)}) %collective-permute-start.2) | collective-permute-done | bytes 8224 | tf_op jit(solution)/shard_map/while/body/eval_jaxpr/ppermute | solution.py:48
  558.9 15.1 %broadcast_multiply_fusion.3 = f32[4,48,2048]{2,1,0:T(8,128)} fusion(f32[4,48]{1,0:T(4,128)S(1)} %mul.190, bf16[4,1024,2048]{2,1,0:T(8,128)(2,1)} %get-tuple-element.393, f32[4,48,1024]{2,1,0:T(8,128)} %fusion.59, bf16[4,48,2048]{2,1,0:T(8,128)(2,1)S(1)} %bitcast.41, bf16[4,2048,1024]{2,1,0:T(8,128)(2,1)} %get-tuple-element.392), kind=kOutput, calls=%fused_computation.12.clone.1 | convolution fusion | flops 1612185600 | bytes 36700928 | tf_op jit(solution)/shard_map/while/body/eval_jaxpr/ecf,efd->ecd/dot_general | solution.py:25
  586.1 10.8 collective-permute-done.2
  628.9 15.1 %broadcast_multiply_fusion.3 = f32[4,48,2048]{2,1,0:T(8,128)} fusion(f32[4,48]{1,0:T(4,128)S(1)} %mul.190, bf16[4,1024,2048]{2,1,0:T(8,128)(2,1)} %get-tuple-element.393, f32[4,48,1024]{2,1,0:T(8,128)} %fusion.59, bf16[4,48,2048]{2,1,0:T(8,128)(2,1)S(1)} %bitcast.41, bf16[4,2048,1024]{2,1,0:T(8,128)(2,1)} %get-tuple-element.392), kind=kOutput, calls=%fused_computation.12.clone.1 | convolution fusion | flops 1612185600 | bytes 36700928 | tf_op jit(solution)/shard_map/while/body/eval_jaxpr/ecf,efd->ecd/dot_general | solution.py:25
  656.2 11.3 %collective-permute-done.2 = f32[256,8]{1,0:T(8,128)S(1)} collective-permute-done((f32[256,8]{1,0:T(8,128)}, f32[256,8]{1,0:T(8,128)S(1)}, u32[]{:S(2)}, u32[]{:S(2)}) %collective-permute-start.2) | collective-permute-done | bytes 8224 | tf_op jit(solution)/shard_map/while/body/eval_jaxpr/ppermute | solution.py:48
  699.5 15.1 %broadcast_multiply_fusion.3 = f32[4,48,2048]{2,1,0:T(8,128)} fusion(f32[4,48]{1,0:T(4,128)S(1)} %mul.190, bf16[4,1024,2048]{2,1,0:T(8,128)(2,1)} %get-tuple-element.393, f32[4,48,1024]{2,1,0:T(8,128)} %fusion.59, bf16[4,48,2048]{2,1,0:T(8,128)(2,1)S(1)} %bitcast.41, bf16[4,2048,1024]{2,1,0:T(8,128)(2,1)} %get-tuple-element.392), kind=kOutput, calls=%fused_computation.12.clone.1 | convolution fusion | flops 1612185600 | bytes 36700928 | tf_op jit(solution)/shard_map/while/body/eval_jaxpr/ecf,efd->ecd/dot_general | solution.py:25
  726.2 11.3 %collective-permute-done.2 = f32[256,8]{1,0:T(8,128)S(1)} collective-permute-done((f32[256,8]{1,0:T(8,128)}, f32[256,8]{1,0:T(8,128)S(1)}, u32[]{:S(2)}, u32[]{:S(2)}) %collective-permute-start.2) | collective-permute-done | bytes 8224 | tf_op jit(solution)/shard_map/while/body/eval_jaxpr/ppermute | solution.py:48
  769.5 15.1 %broadcast_multiply_fusion.3 = f32[4,48,2048]{2,1,0:T(8,128)} fusion(f32[4,48]{1,0:T(4,128)S(1)} %mul.190, bf16[4,1024,2048]{2,1,0:T(8,128)(2,1)} %get-tuple-element.393, f32[4,48,1024]{2,1,0:T(8,128)} %fusion.59, bf16[4,48,2048]{2,1,0:T(8,128)(2,1)S(1)} %bitcast.41, bf16[4,2048,1024]{2,1,0:T(8,128)(2,1)} %get-tuple-element.392), kind=kOutput, calls=%fused_computation.12.clone.1 | convolution fusion | flops 1612185600 | bytes 36700928 | tf_op jit(solution)/shard_map/while/body/eval_jaxpr/ecf,efd->ecd/dot_general | solution.py:25
  797.3 10.3 collective-permute-done.2
  839.6 15.1 %broadcast_multiply_fusion.3 = f32[4,48,2048]{2,1,0:T(8,128)} fusion(f32[4,48]{1,0:T(4,128)S(1)} %mul.190, bf16[4,1024,2048]{2,1,0:T(8,128)(2,1)} %get-tuple-element.393, f32[4,48,1024]{2,1,0:T(8,128)} %fusion.59, bf16[4,48,2048]{2,1,0:T(8,128)(2,1)S(1)} %bitcast.41, bf16[4,2048,1024]{2,1,0:T(8,128)(2,1)} %get-tuple-element.392), kind=kOutput, calls=%fused_computation.12.clone.1 | convolution fusion | flops 1612185600 | bytes 36700928 | tf_op jit(solution)/shard_map/while/body/eval_jaxpr/ecf,efd->ecd/dot_general | solution.py:25
  867.3 11.3 %collective-permute-done.2 = f32[256,8]{1,0:T(8,128)S(1)} collective-permute-done((f32[256,8]{1,0:T(8,128)}, f32[256,8]{1,0:T(8,128)S(1)}, u32[]{:S(2)}, u32[]{:S(2)}) %collective-permute-start.2) | collective-permute-done | bytes 8224 | tf_op jit(solution)/shard_map/while/body/eval_jaxpr/ppermute | solution.py:48
  910.7 15.1 %broadcast_multiply_fusion.3 = f32[4,48,2048]{2,1,0:T(8,128)} fusion(f32[4,48]{1,0:T(4,128)S(1)} %mul.190, bf16[4,1024,2048]{2,1,0:T(8,128)(2,1)} %get-tuple-element.393, f32[4,48,1024]{2,1,0:T(8,128)} %fusion.59, bf16[4,48,2048]{2,1,0:T(8,128)(2,1)S(1)} %bitcast.41, bf16[4,2048,1024]{2,1,0:T(8,128)(2,1)} %get-tuple-element.392), kind=kOutput, calls=%fused_computation.12.clone.1 | convolution fusion | flops 1612185600 | bytes 36700928 | tf_op jit(solution)/shard_map/while/body/eval_jaxpr/ecf,efd->ecd/dot_general | solution.py:25
  937.4 11.3 %collective-permute-done.2 = f32[256,8]{1,0:T(8,128)S(1)} collective-permute-done((f32[256,8]{1,0:T(8,128)}, f32[256,8]{1,0:T(8,128)S(1)}, u32[]{:S(2)}, u32[]{:S(2)}) %collective-permute-start.2) | collective-permute-done | bytes 8224 | tf_op jit(solution)/shard_map/while/body/eval_jaxpr/ppermute | solution.py:48
  980.7 15.1 %broadcast_multiply_fusion.3 = f32[4,48,2048]{2,1,0:T(8,128)} fusion(f32[4,48]{1,0:T(4,128)S(1)} %mul.190, bf16[4,1024,2048]{2,1,0:T(8,128)(2,1)} %get-tuple-element.393, f32[4,48,1024]{2,1,0:T(8,128)} %fusion.59, bf16[4,48,2048]{2,1,0:T(8,128)(2,1)S(1)} %bitcast.41, bf16[4,2048,1024]{2,1,0:T(8,128)(2,1)} %get-tuple-element.392), kind=kOutput, calls=%fused_computation.12.clone.1 | convolution fusion | flops 1612185600 | bytes 36700928 | tf_op jit(solution)/shard_map/while/body/eval_jaxpr/ecf,efd->ecd/dot_general | solution.py:25
  1007.4 11.3 %collective-permute-done.2 = f32[256,8]{1,0:T(8,128)S(1)} collective-permute-done((f32[256,8]{1,0:T(8,128)}, f32[256,8]{1,0:T(8,128)S(1)}, u32[]{:S(2)}, u32[]{:S(2)}) %collective-permute-start.2) | collective-permute-done | bytes 8224 | tf_op jit(solution)/shard_map/while/body/eval_jaxpr/ppermute | solution.py:48
  1050.7 15.1 %broadcast_multiply_fusion.3 = f32[4,48,2048]{2,1,0:T(8,128)} fusion(f32[4,48]{1,0:T(4,128)S(1)} %mul.190, bf16[4,1024,2048]{2,1,0:T(8,128)(2,1)} %get-tuple-element.393, f32[4,48,1024]{2,1,0:T(8,128)} %fusion.59, bf16[4,48,2048]{2,1,0:T(8,128)(2,1)S(1)} %bitcast.41, bf16[4,2048,1024]{2,1,0:T(8,128)(2,1)} %get-tuple-element.392), kind=kOutput, calls=%fused_computation.12.clone.1 | convolution fusion | flops 1612185600 | bytes 36700928 | tf_op jit(solution)/shard_map/while/body/eval_jaxpr/ecf,efd->ecd/dot_general | solution.py:25
  1074.2 18.1 %convolution_multiply_fusion = f32[4,48,2048]{2,1,0:T(8,128)} fusion(bf16[4,1024,2048]{2,1,0:T(8,128)(2,1)} %get-tuple-element.405, f32[4,48]{1,0:T(4,128)S(1)} %copy-done.3, bf16[4,48,2048]{2,1,0:T(8,128)(2,1)} %bitcast.44, bf16[4,2048,1024]{2,1,0:T(8,128)(2,1)} %get-tuple-element.402, f32[4,48,1024]{2,1,0:T(8,128)} %fusion.28), kind=kOutput, calls=%fused_computation.27 | convolution fusion | flops 1612185600 | bytes 36700928 | tf_op jit(solution)/shard_map/ecf,efd->ecd/dot_general | solution.py:25
  (541 shorter events, 692.6 us)
Async XLA Ops:
  0.0 56.7 %collective-permute-start.5 = (bf16[256,2048]{1,0:T(8,128)(2,1)}, bf16[256,2048]{1,0:T(8,128)(2,1)}, u32[]{:S(2)}, u32[]{:S(2)}) collective-permute-start(bf16[256,2048]{1,0:T(8,128)(2,1)} %param.11), channel_id=1, source_target_pairs={{0,1},{1,2},{2,3},{3,4},{4,5},{5,6},{6,7},{7,8},{8,9},{9,10},{10,1... | collective-permute-start | bytes 3145736 | tf_op jit(solution)/shard_map/ppermute | solution.py:43
  3.2 35.8 %collective-permute-start.6 = (s32[256,8]{0,1:T(8,128)}, s32[256,8]{0,1:T(8,128)S(1)}, u32[]{:S(2)}, u32[]{:S(2)}) collective-permute-start(s32[256,8]{0,1:T(8,128)} %param.12), channel_id=1, source_target_pairs={{0,1},{1,2},{2,3},{3,4},{4,5},{5,6},{6,7},{7,8},{8,9},{9,10},{10,1... | collective-permute-start | bytes 24584 | tf_op jit(solution)/shard_map/ppermute | solution.py:43
  4.0 43.3 %collective-permute-start.7 = (f32[256,8]{1,0:T(8,128)S(1)}, f32[256,8]{1,0:T(8,128)}, u32[]{:S(2)}, u32[]{:S(2)}) collective-permute-start(f32[256,8]{1,0:T(8,128)S(1)} %copy.19), channel_id=1, source_target_pairs={{0,1},{1,2},{2,3},{3,4},{4,5},{5,6},{6,7},{7,8},{8,9},{9,10},{10,1... | collective-permute-start | bytes 24584 | tf_op jit(solution)/shard_map/ppermute | solution.py:43
  6.3 32.7 %collective-permute-start.8 = (s32[256,8]{0,1:T(8,128)}, s32[256,8]{0,1:T(8,128)S(1)}, u32[]{:S(2)}, u32[]{:S(2)}) collective-permute-start(s32[256,8]{0,1:T(8,128)} %param.14), channel_id=1, source_target_pairs={{0,1},{1,2},{2,3},{3,4},{4,5},{5,6},{6,7},{7,8},{8,9},{9,10},{10,1... | collective-permute-start | bytes 24584 | tf_op jit(solution)/shard_map/ppermute | solution.py:43
  89.1 33.5 %collective-permute-start = (bf16[256,2048]{1,0:T(8,128)(2,1)}, bf16[256,2048]{1,0:T(8,128)(2,1)S(1)}, u32[]{:S(2)}, u32[]{:S(2)}) collective-permute-start(bf16[256,2048]{1,0:T(8,128)(2,1)} %get-tuple-element.365), channel_id=1, source_target_pairs={{0,1},{1,2},{2,3},{3,4},{4,5},{5,6},{6,7},{7,8},{8,9},{9,10},{10,1... | collective-permute-start | bytes 3145736 | tf_op jit(solution)/shard_map/while/body/eval_jaxpr/ppermute | solution.py:48
  92.6 60.1 %collective-permute-start.4 = (f32[256,2048]{1,0:T(8,128)}, f32[256,2048]{1,0:T(8,128)S(1)}, u32[]{:S(2)}, u32[]{:S(2)}) collective-permute-start(f32[256,2048]{1,0:T(8,128)} %get-tuple-element.369), channel_id=1, source_target_pairs={{0,1},{1,2},{2,3},{3,4},{4,5},{5,6},{6,7},{7,8},{8,9},{9,10},{10,1... | collective-permute-start | bytes 6291464 | tf_op jit(solution)/shard_map/while/body/eval_jaxpr/ppermute | solution.py:48
  161.2 31.4 %collective-permute-start = (bf16[256,2048]{1,0:T(8,128)(2,1)}, bf16[256,2048]{1,0:T(8,128)(2,1)S(1)}, u32[]{:S(2)}, u32[]{:S(2)}) collective-permute-start(bf16[256,2048]{1,0:T(8,128)(2,1)} %get-tuple-element.365), channel_id=1, source_target_pairs={{0,1},{1,2},{2,3},{3,4},{4,5},{5,6},{6,7},{7,8},{8,9},{9,10},{10,1... | collective-permute-start | bytes 3145736 | tf_op jit(solution)/shard_map/while/body/eval_jaxpr/ppermute | solution.py:48
  162.5 60.2 %collective-permute-start.4 = (f32[256,2048]{1,0:T(8,128)}, f32[256,2048]{1,0:T(8,128)S(1)}, u32[]{:S(2)}, u32[]{:S(2)}) collective-permute-start(f32[256,2048]{1,0:T(8,128)} %get-tuple-element.369), channel_id=1, source_target_pairs={{0,1},{1,2},{2,3},{3,4},{4,5},{5,6},{6,7},{7,8},{8,9},{9,10},{10,1... | collective-permute-start | bytes 6291464 | tf_op jit(solution)/shard_map/while/body/eval_jaxpr/ppermute | solution.py:48
  231.1 31.4 %collective-permute-start = (bf16[256,2048]{1,0:T(8,128)(2,1)}, bf16[256,2048]{1,0:T(8,128)(2,1)S(1)}, u32[]{:S(2)}, u32[]{:S(2)}) collective-permute-start(bf16[256,2048]{1,0:T(8,128)(2,1)} %get-tuple-element.365), channel_id=1, source_target_pairs={{0,1},{1,2},{2,3},{3,4},{4,5},{5,6},{6,7},{7,8},{8,9},{9,10},{10,1... | collective-permute-start | bytes 3145736 | tf_op jit(solution)/shard_map/while/body/eval_jaxpr/ppermute | solution.py:48
  232.5 60.2 %collective-permute-start.4 = (f32[256,2048]{1,0:T(8,128)}, f32[256,2048]{1,0:T(8,128)S(1)}, u32[]{:S(2)}, u32[]{:S(2)}) collective-permute-start(f32[256,2048]{1,0:T(8,128)} %get-tuple-element.369), channel_id=1, source_target_pairs={{0,1},{1,2},{2,3},{3,4},{4,5},{5,6},{6,7},{7,8},{8,9},{9,10},{10,1... | collective-permute-start | bytes 6291464 | tf_op jit(solution)/shard_map/while/body/eval_jaxpr/ppermute | solution.py:48
  301.2 32.6 %collective-permute-start = (bf16[256,2048]{1,0:T(8,128)(2,1)}, bf16[256,2048]{1,0:T(8,128)(2,1)S(1)}, u32[]{:S(2)}, u32[]{:S(2)}) collective-permute-start(bf16[256,2048]{1,0:T(8,128)(2,1)} %get-tuple-element.365), channel_id=1, source_target_pairs={{0,1},{1,2},{2,3},{3,4},{4,5},{5,6},{6,7},{7,8},{8,9},{9,10},{10,1... | collective-permute-start | bytes 3145736 | tf_op jit(solution)/shard_map/while/body/eval_jaxpr/ppermute | solution.py:48
  303.7 60.2 %collective-permute-start.4 = (f32[256,2048]{1,0:T(8,128)}, f32[256,2048]{1,0:T(8,128)S(1)}, u32[]{:S(2)}, u32[]{:S(2)}) collective-permute-start(f32[256,2048]{1,0:T(8,128)} %get-tuple-element.369), channel_id=1, source_target_pairs={{0,1},{1,2},{2,3},{3,4},{4,5},{5,6},{6,7},{7,8},{8,9},{9,10},{10,1... | collective-permute-start | bytes 6291464 | tf_op jit(solution)/shard_map/while/body/eval_jaxpr/ppermute | solution.py:48
  372.3 31.5 %collective-permute-start = (bf16[256,2048]{1,0:T(8,128)(2,1)}, bf16[256,2048]{1,0:T(8,128)(2,1)S(1)}, u32[]{:S(2)}, u32[]{:S(2)}) collective-permute-start(bf16[256,2048]{1,0:T(8,128)(2,1)} %get-tuple-element.365), channel_id=1, source_target_pairs={{0,1},{1,2},{2,3},{3,4},{4,5},{5,6},{6,7},{7,8},{8,9},{9,10},{10,1... | collective-permute-start | bytes 3145736 | tf_op jit(solution)/shard_map/while/body/eval_jaxpr/ppermute | solution.py:48
  373.7 60.2 %collective-permute-start.4 = (f32[256,2048]{1,0:T(8,128)}, f32[256,2048]{1,0:T(8,128)S(1)}, u32[]{:S(2)}, u32[]{:S(2)}) collective-permute-start(f32[256,2048]{1,0:T(8,128)} %get-tuple-element.369), channel_id=1, source_target_pairs={{0,1},{1,2},{2,3},{3,4},{4,5},{5,6},{6,7},{7,8},{8,9},{9,10},{10,1... | collective-permute-start | bytes 6291464 | tf_op jit(solution)/shard_map/while/body/eval_jaxpr/ppermute | solution.py:48
  442.4 31.5 %collective-permute-start = (bf16[256,2048]{1,0:T(8,128)(2,1)}, bf16[256,2048]{1,0:T(8,128)(2,1)S(1)}, u32[]{:S(2)}, u32[]{:S(2)}) collective-permute-start(bf16[256,2048]{1,0:T(8,128)(2,1)} %get-tuple-element.365), channel_id=1, source_target_pairs={{0,1},{1,2},{2,3},{3,4},{4,5},{5,6},{6,7},{7,8},{8,9},{9,10},{10,1... | collective-permute-start | bytes 3145736 | tf_op jit(solution)/shard_map/while/body/eval_jaxpr/ppermute | solution.py:48
  443.8 60.2 %collective-permute-start.4 = (f32[256,2048]{1,0:T(8,128)}, f32[256,2048]{1,0:T(8,128)S(1)}, u32[]{:S(2)}, u32[]{:S(2)}) collective-permute-start(f32[256,2048]{1,0:T(8,128)} %get-tuple-element.369), channel_id=1, source_target_pairs={{0,1},{1,2},{2,3},{3,4},{4,5},{5,6},{6,7},{7,8},{8,9},{9,10},{10,1... | collective-permute-start | bytes 6291464 | tf_op jit(solution)/shard_map/while/body/eval_jaxpr/ppermute | solution.py:48
  512.4 31.5 %collective-permute-start = (bf16[256,2048]{1,0:T(8,128)(2,1)}, bf16[256,2048]{1,0:T(8,128)(2,1)S(1)}, u32[]{:S(2)}, u32[]{:S(2)}) collective-permute-start(bf16[256,2048]{1,0:T(8,128)(2,1)} %get-tuple-element.365), channel_id=1, source_target_pairs={{0,1},{1,2},{2,3},{3,4},{4,5},{5,6},{6,7},{7,8},{8,9},{9,10},{10,1... | collective-permute-start | bytes 3145736 | tf_op jit(solution)/shard_map/while/body/eval_jaxpr/ppermute | solution.py:48
  513.8 60.2 %collective-permute-start.4 = (f32[256,2048]{1,0:T(8,128)}, f32[256,2048]{1,0:T(8,128)S(1)}, u32[]{:S(2)}, u32[]{:S(2)}) collective-permute-start(f32[256,2048]{1,0:T(8,128)} %get-tuple-element.369), channel_id=1, source_target_pairs={{0,1},{1,2},{2,3},{3,4},{4,5},{5,6},{6,7},{7,8},{8,9},{9,10},{10,1... | collective-permute-start | bytes 6291464 | tf_op jit(solution)/shard_map/while/body/eval_jaxpr/ppermute | solution.py:48
  582.4 31.5 %collective-permute-start = (bf16[256,2048]{1,0:T(8,128)(2,1)}, bf16[256,2048]{1,0:T(8,128)(2,1)S(1)}, u32[]{:S(2)}, u32[]{:S(2)}) collective-permute-start(bf16[256,2048]{1,0:T(8,128)(2,1)} %get-tuple-element.365), channel_id=1, source_target_pairs={{0,1},{1,2},{2,3},{3,4},{4,5},{5,6},{6,7},{7,8},{8,9},{9,10},{10,1... | collective-permute-start | bytes 3145736 | tf_op jit(solution)/shard_map/while/body/eval_jaxpr/ppermute | solution.py:48
  583.8 60.2 %collective-permute-start.4 = (f32[256,2048]{1,0:T(8,128)}, f32[256,2048]{1,0:T(8,128)S(1)}, u32[]{:S(2)}, u32[]{:S(2)}) collective-permute-start(f32[256,2048]{1,0:T(8,128)} %get-tuple-element.369), channel_id=1, source_target_pairs={{0,1},{1,2},{2,3},{3,4},{4,5},{5,6},{6,7},{7,8},{8,9},{9,10},{10,1... | collective-permute-start | bytes 6291464 | tf_op jit(solution)/shard_map/while/body/eval_jaxpr/ppermute | solution.py:48
  652.5 32.0 %collective-permute-start = (bf16[256,2048]{1,0:T(8,128)(2,1)}, bf16[256,2048]{1,0:T(8,128)(2,1)S(1)}, u32[]{:S(2)}, u32[]{:S(2)}) collective-permute-start(bf16[256,2048]{1,0:T(8,128)(2,1)} %get-tuple-element.365), channel_id=1, source_target_pairs={{0,1},{1,2},{2,3},{3,4},{4,5},{5,6},{6,7},{7,8},{8,9},{9,10},{10,1... | collective-permute-start | bytes 3145736 | tf_op jit(solution)/shard_map/while/body/eval_jaxpr/ppermute | solution.py:48
  654.4 60.2 %collective-permute-start.4 = (f32[256,2048]{1,0:T(8,128)}, f32[256,2048]{1,0:T(8,128)S(1)}, u32[]{:S(2)}, u32[]{:S(2)}) collective-permute-start(f32[256,2048]{1,0:T(8,128)} %get-tuple-element.369), channel_id=1, source_target_pairs={{0,1},{1,2},{2,3},{3,4},{4,5},{5,6},{6,7},{7,8},{8,9},{9,10},{10,1... | collective-permute-start | bytes 6291464 | tf_op jit(solution)/shard_map/while/body/eval_jaxpr/ppermute | solution.py:48
  723.0 31.5 %collective-permute-start = (bf16[256,2048]{1,0:T(8,128)(2,1)}, bf16[256,2048]{1,0:T(8,128)(2,1)S(1)}, u32[]{:S(2)}, u32[]{:S(2)}) collective-permute-start(bf16[256,2048]{1,0:T(8,128)(2,1)} %get-tuple-element.365), channel_id=1, source_target_pairs={{0,1},{1,2},{2,3},{3,4},{4,5},{5,6},{6,7},{7,8},{8,9},{9,10},{10,1... | collective-permute-start | bytes 3145736 | tf_op jit(solution)/shard_map/while/body/eval_jaxpr/ppermute | solution.py:48
  724.4 60.2 %collective-permute-start.4 = (f32[256,2048]{1,0:T(8,128)}, f32[256,2048]{1,0:T(8,128)S(1)}, u32[]{:S(2)}, u32[]{:S(2)}) collective-permute-start(f32[256,2048]{1,0:T(8,128)} %get-tuple-element.369), channel_id=1, source_target_pairs={{0,1},{1,2},{2,3},{3,4},{4,5},{5,6},{6,7},{7,8},{8,9},{9,10},{10,1... | collective-permute-start | bytes 6291464 | tf_op jit(solution)/shard_map/while/body/eval_jaxpr/ppermute | solution.py:48
  793.1 31.5 %collective-permute-start = (bf16[256,2048]{1,0:T(8,128)(2,1)}, bf16[256,2048]{1,0:T(8,128)(2,1)S(1)}, u32[]{:S(2)}, u32[]{:S(2)}) collective-permute-start(bf16[256,2048]{1,0:T(8,128)(2,1)} %get-tuple-element.365), channel_id=1, source_target_pairs={{0,1},{1,2},{2,3},{3,4},{4,5},{5,6},{6,7},{7,8},{8,9},{9,10},{10,1... | collective-permute-start | bytes 3145736 | tf_op jit(solution)/shard_map/while/body/eval_jaxpr/ppermute | solution.py:48
  794.4 60.2 %collective-permute-start.4 = (f32[256,2048]{1,0:T(8,128)}, f32[256,2048]{1,0:T(8,128)S(1)}, u32[]{:S(2)}, u32[]{:S(2)}) collective-permute-start(f32[256,2048]{1,0:T(8,128)} %get-tuple-element.369), channel_id=1, source_target_pairs={{0,1},{1,2},{2,3},{3,4},{4,5},{5,6},{6,7},{7,8},{8,9},{9,10},{10,1... | collective-permute-start | bytes 6291464 | tf_op jit(solution)/shard_map/while/body/eval_jaxpr/ppermute | solution.py:48
  863.1 32.5 %collective-permute-start = (bf16[256,2048]{1,0:T(8,128)(2,1)}, bf16[256,2048]{1,0:T(8,128)(2,1)S(1)}, u32[]{:S(2)}, u32[]{:S(2)}) collective-permute-start(bf16[256,2048]{1,0:T(8,128)(2,1)} %get-tuple-element.365), channel_id=1, source_target_pairs={{0,1},{1,2},{2,3},{3,4},{4,5},{5,6},{6,7},{7,8},{8,9},{9,10},{10,1... | collective-permute-start | bytes 3145736 | tf_op jit(solution)/shard_map/while/body/eval_jaxpr/ppermute | solution.py:48
  865.5 60.2 %collective-permute-start.4 = (f32[256,2048]{1,0:T(8,128)}, f32[256,2048]{1,0:T(8,128)S(1)}, u32[]{:S(2)}, u32[]{:S(2)}) collective-permute-start(f32[256,2048]{1,0:T(8,128)} %get-tuple-element.369), channel_id=1, source_target_pairs={{0,1},{1,2},{2,3},{3,4},{4,5},{5,6},{6,7},{7,8},{8,9},{9,10},{10,1... | collective-permute-start | bytes 6291464 | tf_op jit(solution)/shard_map/while/body/eval_jaxpr/ppermute | solution.py:48
  934.2 31.5 %collective-permute-start = (bf16[256,2048]{1,0:T(8,128)(2,1)}, bf16[256,2048]{1,0:T(8,128)(2,1)S(1)}, u32[]{:S(2)}, u32[]{:S(2)}) collective-permute-start(bf16[256,2048]{1,0:T(8,128)(2,1)} %get-tuple-element.365), channel_id=1, source_target_pairs={{0,1},{1,2},{2,3},{3,4},{4,5},{5,6},{6,7},{7,8},{8,9},{9,10},{10,1... | collective-permute-start | bytes 3145736 | tf_op jit(solution)/shard_map/while/body/eval_jaxpr/ppermute | solution.py:48
  935.6 60.2 %collective-permute-start.4 = (f32[256,2048]{1,0:T(8,128)}, f32[256,2048]{1,0:T(8,128)S(1)}, u32[]{:S(2)}, u32[]{:S(2)}) collective-permute-start(f32[256,2048]{1,0:T(8,128)} %get-tuple-element.369), channel_id=1, source_target_pairs={{0,1},{1,2},{2,3},{3,4},{4,5},{5,6},{6,7},{7,8},{8,9},{9,10},{10,1... | collective-permute-start | bytes 6291464 | tf_op jit(solution)/shard_map/while/body/eval_jaxpr/ppermute | solution.py:48
  1004.2 31.5 %collective-permute-start = (bf16[256,2048]{1,0:T(8,128)(2,1)}, bf16[256,2048]{1,0:T(8,128)(2,1)S(1)}, u32[]{:S(2)}, u32[]{:S(2)}) collective-permute-start(bf16[256,2048]{1,0:T(8,128)(2,1)} %get-tuple-element.365), channel_id=1, source_target_pairs={{0,1},{1,2},{2,3},{3,4},{4,5},{5,6},{6,7},{7,8},{8,9},{9,10},{10,1... | collective-permute-start | bytes 3145736 | tf_op jit(solution)/shard_map/while/body/eval_jaxpr/ppermute | solution.py:48
  1005.6 60.2 %collective-permute-start.4 = (f32[256,2048]{1,0:T(8,128)}, f32[256,2048]{1,0:T(8,128)S(1)}, u32[]{:S(2)}, u32[]{:S(2)}) collective-permute-start(f32[256,2048]{1,0:T(8,128)} %get-tuple-element.369), channel_id=1, source_target_pairs={{0,1},{1,2},{2,3},{3,4},{4,5},{5,6},{6,7},{7,8},{8,9},{9,10},{10,1... | collective-permute-start | bytes 6291464 | tf_op jit(solution)/shard_map/while/body/eval_jaxpr/ppermute | solution.py:48
  (75 other events, 1505.1 us)
where the time goes:
time: 1110 us; the launch traced here: 1100 us
  matrix products  398 us (36%)
  local copies, waits for them, and re-layouts  360 us (32%)
  waiting for transfers between devices  161 us (15%)
  other arithmetic  93.1 us (8%)
  starting transfers between devices  88.8 us (8%)
    dot_general x16, matrix products, local_share(): jnp.einsum('ecf,efd->ecd', hidden, w_down, preferred_element_type=jnp.flo...  243 us
    ppermute x70, waiting for transfers between devices, pass_on(): visitor, accum = lax.ppermute((visitor, accum), 'ep', next_perm)  156 us
    dot_general x16, matrix products, local_share(): jnp.einsum('ecd,edf->ecf', dispatched, w_gate, preferred_element_type=jnp...  155 us
    scatter x16, local copies, waits for them, and re-layouts, local_share(): jnp.zeros((num_local * shard_cap,), jnp.float32).at[flat_slot]  129 us
    scatter x16, local copies, waits for them, and re-layouts, local_share(): jnp.full((num_local * shard_cap,), tok_dev, jnp.int32).at[flat_slot]  129 us
    ppermute x70, starting transfers between devices, pass_on(): visitor, accum = lax.ppermute((visitor, accum), 'ep', next_perm)  80.8 us
    scatter-add x16, other arithmetic, local_share(): jnp.zeros((tok_dev, token_blk.shape[1]), jnp.float32).at[slot_token]  72.8 us
    while x126, local copies, waits for them, and re-layouts  55 us
  transfers between devices with their start and end apart: 75, of which 15 were waited for; matrix products, arithmetic and copies ran while one was open for 65% of the time, Pallas kernels for 0%

commit v1 on v0

v1 whole, which is shorter than its diff:
```python
import functools

import jax
import jax.numpy as jnp
from jax import lax
from jax.experimental import pallas as pl
from jax.experimental.pallas import tpu as pltpu
from jax.sharding import PartitionSpec as P

CAP_NUM = 3
CAP_DEN = 2
COLS = 256
AG_CHUNKS = 2
SIB_SLOTS = 4
MESH = pl.DeviceIdType.MESH
BF16 = jnp.bfloat16
F32 = jnp.float32


def moe_kernel(cfg, tok_in, meta_in, wg, wu, wd, out,
               tok, meta, ring, sib_in, sib_out, own, wbuf, xbuf, hbuf, obuf, ptbuf, sgbuf,
               local_sem, w_sem, ag_s, ag_r, agm_s, agm_r, sb_s, sb_r, sbm_s, sbm_r, own_s, own_r,
               rs_s, rs_r, ss_s, ss_r, credit):
    n, cap, spad, n_w = cfg
    rows, d_model = tok_in.shape
    n_exp, _, d_ff = wg.shape
    chips = n // 2
    far = chips // 2
    half = rows // 2
    piece = half // AG_CHUNKS
    n_d = d_model // COLS
    n_f = d_ff // COLS
    slots = n_exp * spad
    up_loads = 2 * n_exp * n_f
    loads = up_loads + n_d * n_exp // 2
    total_chunks = (far + 1) * n_d
    a_slot, b_slot = 0, far + 1

    me = lax.axis_index('ep')
    chip, core = me // 2, me % 2
    other = 1 - core

    def place(chip_num, core_num):
        return ((chip_num + chips) % chips) * 2 + core_num

    sib = chip * 2 + other
    side = (place(chip + 1, core), place(chip - 1, core))
    sign = (1, -1)

    def load_up(idx, slot, start):
        step = idx // 2
        exp_num, col = step // n_f, pl.multiple_of((step % n_f) * COLS, COLS)
        start(pltpu.make_async_copy(wg.at[exp_num, :, pl.ds(col, COLS)], wbuf.at[slot], w_sem.at[slot, 0]))
        start(pltpu.make_async_copy(wu.at[exp_num, :, pl.ds(col, COLS)], wbuf.at[slot + 1], w_sem.at[slot + 1, 0]))

    def load_down(idx, slot, start):
        col, pair = pl.multiple_of((idx // (n_exp // 2)) * COLS, COLS), idx % (n_exp // 2)
        for k in range(2):
            start(pltpu.make_async_copy(wd.at[pair * 2 + k, :, pl.ds(col, COLS)], wbuf.at[slot, pl.ds(k * d_ff, d_ff)], w_sem.at[slot, k]))

    begin = lambda copy: copy.start()
    finish = lambda copy: copy.wait()

    def part_rows(way, kind, ck):
        upper = (way == 0) == (kind == 1)
        return pl.ds((half if upper else 0) + ck * piece, piece)

    def ag(way, kind, hop, ck, arriving):
        origin = place(chip - sign[way] * (hop if arriving else hop - 1), core)
        if isinstance(ck, int):
            view = tok.at[origin, part_rows(way, kind, ck)]
        else:
            base = half if (way == 0) == (kind == 1) else 0
            view = tok.at[origin, pl.ds(pl.multiple_of(base + ck * piece, piece), piece)]
        copy = pltpu.make_async_remote_copy(view, view, ag_s.at[way, kind, hop - 1, ck], ag_r.at[way, kind, hop - 1, ck], device_id={'ep': side[way]}, device_id_type=MESH)
        return copy, origin, view

    def ag_meta(way, hop, arriving):
        origin = place(chip - sign[way] * (hop if arriving else hop - 1), core)
        view = meta.at[origin]
        copy = pltpu.make_async_remote_copy(view, view, agm_s.at[way, hop - 1], agm_r.at[way, hop - 1], device_id={'ep': side[way]}, device_id_type=MESH)
        return copy, origin, view

    def to_sib(view, send_sem, recv_sem):
        return pltpu.make_async_remote_copy(view, view, send_sem, recv_sem, device_id={'ep': sib}, device_id_type=MESH)

    def sib_view(way, kind, hop, ck, core_num):
        origin = place(chip - sign[way] * hop, core_num)
        base = half if (way == 0) == (kind == 1) else 0
        return tok.at[origin, pl.ds(pl.multiple_of(base + ck * piece, piece), piece)]

    def sib_msg(way, kind, hop, ck, core_num):
        return to_sib(sib_view(way, kind, hop, ck, core_num), sb_s.at[way, kind, hop - 1, ck], sb_r.at[way, kind, hop - 1, ck])

    def sib_meta(way, hop, core_num):
        return to_sib(meta.at[place(chip - sign[way] * hop, core_num)], sbm_s.at[way, hop - 1], sbm_r.at[way, hop - 1])

    meta_hops = (far, far - 1)

    local = (pltpu.make_async_copy(tok_in, tok.at[me], local_sem.at[0]), pltpu.make_async_copy(meta_in, meta.at[me], local_sem.at[1]))
    for copy in local:
        copy.start()
    for idx in range(0, n_w, 2):
        load_up(jnp.int32(idx), idx, begin)
    barrier = pltpu.get_barrier_semaphore()
    for dev in (side[0], side[1], sib):
        pl.semaphore_signal(barrier, inc=1, device_id={'ep': dev}, device_id_type=MESH)
    pl.semaphore_wait(barrier, 3)
    for copy in local:
        copy.wait()

    own_tok = lambda core_num: to_sib(tok.at[place(chip, core_num)], own_s.at[0], own_r.at[0])
    own_meta = lambda core_num: to_sib(meta.at[place(chip, core_num)], own_s.at[1], own_r.at[1])
    for way in range(2):
        ag_meta(way, 1, False)[0].start()
    for ck in range(AG_CHUNKS):
        for way in range(2):
            ag(way, 0, 1, ck, False)[0].start()
    own_meta(core).start()
    own_tok(core).start()
    obuf[...] = jnp.zeros_like(obuf)
    for hop in range(1, far + 1):
        for way in range(2):
            if hop <= meta_hops[way]:
                ag_meta(way, hop, True)[0].wait_recv()
                if hop < meta_hops[way]:
                    ag_meta(way, hop + 1, False)[0].start()
                sib_meta(way, hop, core).start()
        for ck in range(AG_CHUNKS):
            for way in range(2):
                ag(way, 0, hop, ck, True)[0].wait_recv()
                if hop < far:
                    ag(way, 0, hop + 1, ck, False)[0].start()
                sib_msg(way, 0, hop, ck, core).start()
        if hop == far - 1:
            for ck in range(AG_CHUNKS):
                for way in range(2):
                    ag(way, 1, 1, ck, False)[0].start()

    def second_half_event(event):
        hop, ck = event // AG_CHUNKS + 1, event % AG_CHUNKS
        for way in range(2):
            ag(way, 1, hop, ck, True)[0].wait_recv()

            @pl.when(hop < far - 1)
            def _():
                ag(way, 1, hop + 1, ck, False)[0].start()
            sib_msg(way, 1, hop, ck, core).start()

    n_events = (far - 1) * AG_CHUNKS

    def rs(way, slot, d):
        return pltpu.make_async_remote_copy(ring.at[way, slot, d], ring.at[way, slot + 1, d], rs_s.at[way, slot, d], rs_r.at[way, slot + 1, d], device_id={'ep': side[way]}, device_id_type=MESH)

    def rs_wait(way, slot, d):
        pltpu.make_async_remote_copy(ring.at[way, slot, d], ring.at[way, slot, d], rs_s.at[way, slot, d], rs_r.at[way, slot, d], device_id={'ep': side[way]}, device_id_type=MESH).wait_recv()

    lane_rows = (pl.ds(0, half), pl.ds(half, half))

    def phase(dist, order, shards, last=False, events=False):
        width = shards // 2
        m_rows = shards * cap

        def shard_place(num):
            which = num % width
            step = dist if width == 1 else dist * (1 - 2 * which)
            return place(chip + step, jnp.where(num < width, core, other))

        def gather(num, carry):
            shard = shard_place(num)
            base = (me * n_exp * cap).astype(F32)
            row_num = lax.broadcasted_iota(jnp.int32, (slots, rows), 0)
            in_exp = row_num % spad
            want = jnp.where(in_exp < cap, (row_num // spad) * cap + in_exp, -7).astype(F32)
            codes = meta[shard, pl.ds(0, 8), :] - base
            gates = meta[shard, pl.ds(8, 8), :]
            hot = jnp.zeros((slots, rows), F32)
            gate = jnp.zeros((slots, rows), F32)
            for j in range(8):
                same = want == codes[j:j + 1, :]
                hot = jnp.where(same, 1.0, hot)
                gate = jnp.where(same, gates[j:j + 1, :], gate)
            slot_gate = jnp.broadcast_to(jnp.sum(gate, axis=1, keepdims=True), (slots, 128))
            first = pl.multiple_of(num * cap, 16)
            for e in range(n_exp):
                sgbuf[e, pl.ds(first, cap), :] = slot_gate[e * spad:e * spad + cap]
            ptbuf[num] = hot.T.astype(BF16)
            pick = hot.astype(BF16)
            for c in range(d_model // COLS):
                got = jnp.dot(pick, tok[shard, :, pl.ds(c * COLS, COLS)], preferred_element_type=F32).astype(BF16)
                for e in range(n_exp):
                    xbuf[e, pl.ds(first, cap), pl.ds(c * COLS, COLS)] = got[e * spad:e * spad + cap]
            return carry

        lax.fori_loop(0, shards, gather, 0)

        def up_step(step, carry):
            idx = step * 2
            slot = idx % n_w
            load_up(idx, slot, finish)
            e, col = step // n_f, pl.multiple_of((step % n_f) * COLS, COLS)
            x = xbuf[e, pl.ds(0, m_rows), :]
            a = jnp.dot(x, wbuf[slot], preferred_element_type=F32)
            u = jnp.dot(x, wbuf[slot + 1], preferred_element_type=F32)
            hbuf[e, pl.ds(0, m_rows), pl.ds(col, COLS)] = (jax.nn.silu(a) * u).astype(BF16)

            @pl.when(idx + n_w < up_loads)
            def _():
                load_up(idx + n_w, slot, begin)

            @pl.when(idx + n_w >= up_loads)
            def _():
                for k in range(2):
                    load_down(idx + n_w + k - up_loads, slot + k, begin)
            if events:
                every = max(n_exp * n_f // max(n_events - 2, 1), 1)

                @pl.when((step % every == every - 1) & (step // every < n_events - 2))
                def _():
                    second_half_event(step // every)
            return carry

        lax.fori_loop(0, n_exp * n_f, up_step, 0)

        def sib_share(d, waiting=False):
            count = order * n_d + d
            return pltpu.make_async_remote_copy(sib_out.at[d % 2, pl.ds(0, width)], sib_in.at[count % SIB_SLOTS, pl.ds(0, width)], ss_s.at[d % 2], ss_r.at[count % SIB_SLOTS], device_id={'ep': sib}, device_id_type=MESH)

        def close(d):
            count = order * n_d + d
            slot = count % SIB_SLOTS
            sib_share(d).wait_recv()
            mine = lambda i, r: own[d % 2, i, lane_rows[r], :] + sib_in[slot, i, lane_rows[r], :]
            if last:
                for way in range(2):
                    rs_wait(way, a_slot + far, d)
                    rs_wait(way, b_slot + far - 1, d)
                for r in range(2):
                    total = mine(0, r) + ring[r, a_slot + far, d] + ring[1 - r, b_slot + far - 1, d]
                    out[lane_rows[r], pl.ds(pl.multiple_of(d * COLS, COLS), COLS)] = total.astype(BF16)
            elif width == 1:
                for way in range(2):
                    ring[way, a_slot, d] = mine(0, way)
                    rs(way, a_slot, d).start()
            else:
                b_now = b_slot + far - 1 - dist
                a_now = a_slot + far - dist

                @pl.when(dist == far - 1)
                def _():
                    for way in range(2):
                        ring[way, b_slot, d] = mine(way, 1 - way)

                @pl.when(dist != far - 1)
                def _():
                    for way in range(2):
                        rs_wait(way, b_now, d)
                        ring[way, b_now, d] += mine(way, 1 - way)
                for way in range(2):
                    rs(way, b_now, d).start()
                for way in range(2):
                    rs_wait(way, a_now, d)
                    ring[way, a_now, d] += mine(way, way)
                    rs(way, a_now, d).start()

            @pl.when(count < total_chunks - SIB_SLOTS)
            def _():
                pl.semaphore_signal(credit, inc=1, device_id={'ep': sib}, device_id_type=MESH)

        def down_step(d, carry):
            for pair in range(n_exp // 2):
                idx = d * (n_exp // 2) + pair
                slot = (up_loads + idx) % n_w
                load_down(idx, slot, finish)
                for k in range(2):
                    e = pair * 2 + k
                    o = jnp.dot(hbuf[e, pl.ds(0, m_rows), :], wbuf[slot, pl.ds(k * d_ff, d_ff), :], preferred_element_type=F32)
                    g = sgbuf[e, pl.ds(0, m_rows), :]
                    o = o * jnp.concatenate([g] * (COLS // 128), axis=1)
                    for p in range(3):
                        cut = o.astype(BF16)
                        o = o - cut.astype(F32)
                        for i in range(shards):
                            obuf[i, pl.ds(p * slots + e * spad, cap), :] = cut[i * cap:(i + 1) * cap]

                @pl.when(up_loads + idx + n_w < loads)
                def _():
                    load_down(idx + n_w, slot, begin)
                if not last:
                    @pl.when((up_loads + idx + n_w >= loads) & ((up_loads + idx + n_w - loads) % 2 == 1))
                    def _():
                        load_up(up_loads + idx + n_w - loads - 1, slot - 1, begin)

            @pl.when(d >= 2)
            def _():
                sib_share(d).wait_send()

            @pl.when(order * n_d + d >= SIB_SLOTS)
            def _():
                pl.semaphore_wait(credit, 1)
            for i in list(range(width, shards)) + list(range(width)):
                pt = ptbuf[i]
                share = jnp.dot(pt, obuf[i, pl.ds(0, slots), :], preferred_element_type=F32)
                for p in range(1, 3):
                    share += jnp.dot(pt, obuf[i, pl.ds(p * slots, slots), :], preferred_element_type=F32)
                if i >= width:
                    sib_out[d % 2, i - width] = share
                else:
                    own[d % 2, i] = share
                if i == shards - 1:
                    sib_share(d).start()

            @pl.when(d >= 1)
            def _():
                close(d - 1)
            if events:
                for k in range(2):
                    @pl.when(d == (k + 1) * n_d // 2 - 1)
                    def _():
                        second_half_event(n_events - 2 + k)
            return carry

        lax.fori_loop(0, n_d, down_step, 0)
        close(jnp.int32(n_d - 1))
        for d in range(n_d - 2, n_d):
            sib_share(d).wait_send()

    for way in range(2):
        if far <= meta_hops[way]:
            sib_meta(way, far, other).wait_recv()
        for ck in range(AG_CHUNKS):
            sib_msg(way, 0, far, ck, other).wait_recv()
    phase(far, 0, 2, events=True)

    def middle(order, carry):
        dist = far - order
        for way in range(2):
            sib_meta(way, dist, other).wait_recv()
            for kind in range(2):
                for ck in range(AG_CHUNKS):
                    sib_msg(way, kind, dist, ck, other).wait_recv()
        phase(dist, order, 4)
        return carry

    lax.fori_loop(1, far, middle, 0)
    own_meta(other).wait_recv()
    own_tok(other).wait_recv()
    phase(0, far, 2, last=True)

    own_meta(core).wait_send()
    own_tok(core).wait_send()
    for way in range(2):
        for hop in range(1, far + 1):
            if hop <= meta_hops[way]:
                ag_meta(way, hop, False)[0].wait_send()
                sib_meta(way, hop, core).wait_send()
            for kind in range(2):
                if hop <= far - kind:
                    for ck in range(AG_CHUNKS):
                        ag(way, kind, hop, ck, False)[0].wait_send()
                        sib_msg(way, kind, hop, ck, core).wait_send()

        def drain(d, carry):
            for slot in list(range(a_slot, a_slot + far)) + list(range(b_slot, b_slot + far - 1)):
                rs(way, slot, d).wait_send()
            return carry
        lax.fori_loop(0, n_d, drain, 0)


def group_layer(n, tokens, meta, w_gate, w_up, w_down, cap):
    rows, d_model = tokens.shape
    n_exp, _, d_ff = w_gate.shape
    far = n // 4
    spad = (cap + 63) // 64 * 64
    slots = n_exp * spad
    n_d = d_model // COLS
    loads = 2 * n_exp * d_ff // COLS + n_d * n_exp // 2
    n_w = 8 if loads % 8 == 0 else 4
    any_spec = pl.BlockSpec(memory_space=pl.ANY)
    dma = pltpu.SemaphoreType.DMA
    ag_shape = (2, 2, far, AG_CHUNKS)
    return pl.pallas_call(
        functools.partial(moe_kernel, (n, cap, spad, n_w)),
        out_shape=jax.ShapeDtypeStruct((rows, d_model), BF16),
        in_specs=[any_spec] * 5,
        out_specs=pl.BlockSpec(memory_space=pltpu.VMEM),
        scratch_shapes=[
            pltpu.VMEM((n, rows, d_model), BF16),
            pltpu.VMEM((n, 16, rows), F32),
            pltpu.VMEM((2, 2 * far + 1, n_d, rows // 2, COLS), F32),
            pltpu.VMEM((SIB_SLOTS, 2, rows, COLS), F32),
            pltpu.VMEM((2, 2, rows, COLS), F32),
            pltpu.VMEM((2, 2, rows, COLS), F32),
            pltpu.VMEM((n_w, d_model, COLS), BF16),
            pltpu.VMEM((n_exp, 4 * cap, d_model), BF16),
            pltpu.VMEM((n_exp, 4 * cap, d_ff), BF16),
            pltpu.VMEM((4, 3 * slots, COLS), BF16),
            pltpu.VMEM((4, rows, slots), BF16),
            pltpu.VMEM((n_exp, 4 * cap, 128), F32),
            dma((2,)), dma((n_w, 2)),
            dma(ag_shape), dma(ag_shape), dma((2, far)), dma((2, far)),
            dma(ag_shape), dma(ag_shape), dma((2, far)), dma((2, far)),
            dma((2,)), dma((2,)),
            dma((2, 2 * far + 1, n_d)), dma((2, 2 * far + 1, n_d)),
            dma((2,)), dma((SIB_SLOTS,)),
            pltpu.SemaphoreType.REGULAR,
        ],
        compiler_params=pltpu.CompilerParams(collective_id=0, has_side_effects=True, vmem_limit_bytes=67043328),
    )(tokens, meta, w_gate, w_up, w_down)


def solution(mesh):
    group_size = mesh.shape['ep']
    row_spec = P(('dp', 'ep'), None)
    expert_spec = P('ep', None, None)

    def per_device(tokens, expert_ids, gate_wts, slot_ids, w_gate, w_up, w_down):
        rank = lax.axis_index('ep')
        tok_dev, top_k = expert_ids.shape
        cap = CAP_NUM * tok_dev * top_k // (CAP_DEN * w_gate.shape[0] * group_size)
        code = jnp.where(slot_ids >= 0, expert_ids * cap + slot_ids - rank * cap, -1).astype(F32)
        meta = jnp.concatenate([code.T, gate_wts.T], axis=0)
        return group_layer(group_size, tokens, meta, w_gate, w_up, w_down, cap)

    return jax.shard_map(per_device, mesh=mesh, in_specs=(row_spec, row_spec, row_spec, row_spec, expert_spec, expert_spec, expert_spec), out_specs=row_spec, check_vma=False)
```

time: 1110 us -> 259 us (0.23)
  matrix products: 398 us -> 0 us
  local copies, waits for them, and re-layouts: 360 us -> 2.3 us
  Pallas kernels: 0 us -> 255 us
  waiting for transfers between devices: 161 us -> 0 us
  other arithmetic: 93.1 us -> 2.02 us
  starting transfers between devices: 88.8 us -> 0 us
    dot_general x32 -> x0, matrix products: 398 us -> none  [the longest x16 243 us: local_share(): jnp.einsum('ecf,efd->ecd', hidden, w_down, preferred_element_type=jnp.flo...]
    scatter x32 -> x0, local copies, waits for them, and re-layouts: 257 us -> none  [the longest x16 129 us: local_share(): jnp.zeros((num_local * shard_cap,), jnp.float32).at[flat_slot]]
    pallas_call x0 -> x1, Pallas kernels: none -> 255 us  [group_layer(): pl.pallas_call(functools.partial(moe_kernel, (n, cap, spad, n_w)), out_sh...]
    ppermute x75 -> x0, waiting for transfers between devices: 161 us -> none  [the longest x70 156 us: pass_on(): visitor, accum = lax.ppermute((visitor, accum), 'ep', next_perm)]
    ppermute x75 -> x0, starting transfers between devices: 88.8 us -> none  [the longest x70 80.8 us: pass_on(): visitor, accum = lax.ppermute((visitor, accum), 'ep', next_perm)]
    scatter-add x16 -> x0, other arithmetic: 72.8 us -> none  [local_share(): jnp.zeros((tok_dev, token_blk.shape[1]), jnp.float32).at[slot_token]]
    while x126 -> x0, local copies, waits for them, and re-layouts: 55 us -> none
    gather x16 -> x0, local copies, waits for them, and re-layouts: 35.3 us -> none  [local_share(): jnp.take(token_blk, slot_token, axis=0, mode='fill', fill_value=0)]
  transfers between devices with their start and end apart: 75 -> 0, of which waited for: 15 -> 0; matrix products, arithmetic and copies ran while one was open for 65% -> 0% of each run, Pallas kernels for 0% -> 0%
where the time goes in v1:
time: 259 us
  Pallas kernels  255 us (98%)
    pallas_call x1, Pallas kernels, group_layer(): pl.pallas_call(functools.partial(moe_kernel, (n, cap, spad, n_w)), out_sh...  255 us

profile of v1, /device:TPU:21, one launch (start us, length us, event | category | flops | bytes accessed | tf_op | source)
XLA Modules:
  0.0 258.9 jit_solution(4910105062567663234)
XLA Ops:
  0.0 0.7 convert_bitcast_fusion
  0.7 1.3 pad_maximum_fusion.meta_in
  2.0 254.5 %shard_map.73 = bf16[256,2048]{1,0:T(8,128)(2,1)} custom-call(bf16[256,2048]{1,0:T(8,128)(2,1)} %tok_in.1, f32[16,256]{1,0:T(8,128)} %pad_maximum_fusion.meta_in, bf16[4,2048,1024]{2,1,0:T(8,128)(2,1)} %wg.1, bf16[4,2048,1024]{2,1,0:T(8,128)(2,1)} %wu.1, bf16[4,1024,2048]{2,1,0:T(8,128)(2,1)} %wd.1), custom_call_target="tpu_custom_call" | custom-call | tf_op jit(solution)/shard_map/pallas_call | solution.py:382
  256.6 2.3 copy.9

commit v2 on v1

--- a/solution.py
+++ b/solution.py
@@ -17,12 +17,13 @@
 F32 = jnp.float32
 
 
-def moe_kernel(cfg, tok_in, meta_in, wg, wu, wd, out,
-               tok, meta, ring, sib_in, sib_out, own, wbuf, xbuf, hbuf, obuf, ptbuf, sgbuf,
+def moe_kernel(cfg, tok_in, ids_in, gates_in, slots_in, wg, wu, wd, out,
+               tok, meta, raw, ring, sib_in, sib_out, own, wbuf, xbuf, hbuf, obuf, ptbuf, sgbuf,
                local_sem, w_sem, ag_s, ag_r, agm_s, agm_r, sb_s, sb_r, sbm_s, sbm_r, own_s, own_r,
                rs_s, rs_r, ss_s, ss_r, credit):
     n, cap, spad, n_w = cfg
     rows, d_model = tok_in.shape
+    top_k = ids_in.shape[0]
     n_exp, _, d_ff = wg.shape
     chips = n // 2
     far = chips // 2
@@ -97,17 +98,22 @@
 
     meta_hops = (far, far - 1)
 
-    local = (pltpu.make_async_copy(tok_in, tok.at[me], local_sem.at[0]), pltpu.make_async_copy(meta_in, meta.at[me], local_sem.at[1]))
-    for copy in local:
-        copy.start()
-    for idx in range(0, n_w, 2):
-        load_up(jnp.int32(idx), idx, begin)
     barrier = pltpu.get_barrier_semaphore()
     for dev in (side[0], side[1], sib):
         pl.semaphore_signal(barrier, inc=1, device_id={'ep': dev}, device_id_type=MESH)
+    local = (pltpu.make_async_copy(ids_in, raw.at[0], local_sem.at[0]), pltpu.make_async_copy(slots_in, raw.at[1], local_sem.at[1]),
+             pltpu.make_async_copy(gates_in, meta.at[me, pl.ds(top_k, top_k)], local_sem.at[2]), pltpu.make_async_copy(tok_in, tok.at[me], local_sem.at[3]))
+    for copy in local:
+        copy.start()
+    for copy in local[:2]:
+        copy.wait()
+    slot_ids = raw[1]
+    meta[me, pl.ds(0, top_k), :] = jnp.where(slot_ids >= 0, raw[0] * cap + slot_ids - me * cap, -1).astype(F32)
+    for idx in range(0, n_w, 2):
+        load_up(jnp.int32(idx), idx, begin)
+    for copy in local[2:]:
+        copy.wait()
     pl.semaphore_wait(barrier, 3)
-    for copy in local:
-        copy.wait()
 
     own_tok = lambda core_num: to_sib(tok.at[place(chip, core_num)], own_s.at[0], own_r.at[0])
     own_meta = lambda core_num: to_sib(meta.at[place(chip, core_num)], own_s.at[1], own_r.at[1])
@@ -172,11 +178,11 @@
             row_num = lax.broadcasted_iota(jnp.int32, (slots, rows), 0)
             in_exp = row_num % spad
             want = jnp.where(in_exp < cap, (row_num // spad) * cap + in_exp, -7).astype(F32)
-            codes = meta[shard, pl.ds(0, 8), :] - base
-            gates = meta[shard, pl.ds(8, 8), :]
+            codes = meta[shard, pl.ds(0, top_k), :] - base
+            gates = meta[shard, pl.ds(top_k, top_k), :]
             hot = jnp.zeros((slots, rows), F32)
             gate = jnp.zeros((slots, rows), F32)
-            for j in range(8):
+            for j in range(top_k):
                 same = want == codes[j:j + 1, :]
                 hot = jnp.where(same, 1.0, hot)
                 gate = jnp.where(same, gates[j:j + 1, :], gate)
@@ -367,8 +373,9 @@
         lax.fori_loop(0, n_d, drain, 0)
 
 
-def group_layer(n, tokens, meta, w_gate, w_up, w_down, cap):
+def group_layer(n, tokens, ids, gates, slot_ids, w_gate, w_up, w_down, cap):
     rows, d_model = tokens.shape
+    top_k = ids.shape[0]
     n_exp, _, d_ff = w_gate.shape
     far = n // 4
     spad = (cap + 63) // 64 * 64
@@ -381,12 +388,13 @@
     ag_shape = (2, 2, far, AG_CHUNKS)
     return pl.pallas_call(
         functools.partial(moe_kernel, (n, cap, spad, n_w)),
-        out_shape=jax.ShapeDtypeStruct((rows, d_model), BF16),
-        in_specs=[any_spec] * 5,
+        out_shape=pltpu.VMEM((rows, d_model), BF16),
+        in_specs=[any_spec] * 7,
         out_specs=pl.BlockSpec(memory_space=pltpu.VMEM),
         scratch_shapes=[
             pltpu.VMEM((n, rows, d_model), BF16),
-            pltpu.VMEM((n, 16, rows), F32),
+            pltpu.VMEM((n, 2 * top_k, rows), F32),
+            pltpu.VMEM((2, top_k, rows), jnp.int32),
             pltpu.VMEM((2, 2 * far + 1, n_d, rows // 2, COLS), F32),
             pltpu.VMEM((SIB_SLOTS, 2, rows, COLS), F32),
             pltpu.VMEM((2, 2, rows, COLS), F32),
@@ -397,7 +405,7 @@
             pltpu.VMEM((4, 3 * slots, COLS), BF16),
             pltpu.VMEM((4, rows, slots), BF16),
             pltpu.VMEM((n_exp, 4 * cap, 128), F32),
-            dma((2,)), dma((n_w, 2)),
+            dma((4,)), dma((n_w, 2)),
             dma(ag_shape), dma(ag_shape), dma((2, far)), dma((2, far)),
             dma(ag_shape), dma(ag_shape), dma((2, far)), dma((2, far)),
             dma((2,)), dma((2,)),
@@ -405,8 +413,8 @@
             dma((2,)), dma((SIB_SLOTS,)),
             pltpu.SemaphoreType.REGULAR,
         ],
-        compiler_params=pltpu.CompilerParams(collective_id=0, has_side_effects=True, vmem_limit_bytes=67043328),
-    )(tokens, meta, w_gate, w_up, w_down)
+        compiler_params=pltpu.CompilerParams(collective_id=0, has_side_effects=True, vmem_limit_bytes=58 << 20),
+    )(tokens, ids, gates, slot_ids, w_gate, w_up, w_down)
 
 
 def solution(mesh):
@@ -415,11 +423,8 @@
     expert_spec = P('ep', None, None)
 
     def per_device(tokens, expert_ids, gate_wts, slot_ids, w_gate, w_up, w_down):
-        rank = lax.axis_index('ep')
         tok_dev, top_k = expert_ids.shape
         cap = CAP_NUM * tok_dev * top_k // (CAP_DEN * w_gate.shape[0] * group_size)
-        code = jnp.where(slot_ids >= 0, expert_ids * cap + slot_ids - rank * cap, -1).astype(F32)
-        meta = jnp.concatenate([code.T, gate_wts.T], axis=0)
-        return group_layer(group_size, tokens, meta, w_gate, w_up, w_down, cap)
+        return group_layer(group_size, tokens, expert_ids.T, gate_wts.T, slot_ids.T, w_gate, w_up, w_down, cap)
 
     return jax.shard_map(per_device, mesh=mesh, in_specs=(row_spec, row_spec, row_spec, row_spec, expert_spec, expert_spec, expert_spec), out_specs=row_spec, check_vma=False)

time: 259 us -> 253 us (0.977)
  Pallas kernels: 255 us -> 252 us
    pallas_call x1, Pallas kernels: 255 us -> 252 us  [group_layer(): pl.pallas_call(functools.partial(moe_kernel, (n, cap, spad, n_w)), out_sh...]
where the time goes in v2:
time: 253 us
  Pallas kernels  252 us (100%)
    pallas_call x1, Pallas kernels, group_layer(): pl.pallas_call(functools.partial(moe_kernel, (n, cap, spad, n_w)), out_sh...  252 us

profile of v2, /device:TPU:21, one launch (start us, length us, event | category | flops | bytes accessed | tf_op | source)
XLA Modules:
  0.0 252.5 jit_solution(13926928263311084426)
XLA Ops:
  0.0 251.5 %shard_map.73 = bf16[256,2048]{1,0:T(8,128)(2,1)S(1)} custom-call(bf16[256,2048]{1,0:T(8,128)(2,1)} %tok_in.1, s32[8,256]{1,0:T(8,128)} %bitcast.3, f32[8,256]{1,0:T(8,128)} %bitcast.4, s32[8,256]{1,0:T(8,128)} %bitcast.5, bf16[4,2048,1024]{2,1,0:T(8,128)(2,1)} %wg.1, bf16[4,2048,1024]{2,1,0:T(8,128)(2,1)} %wu.1, bf16[4,1024,2048]{2,1,0:T(8,128)(2,1)} %wd.1), custom_call_target="tpu_custom_call" | custom-call | tf_op jit(solution)/shard_map/pallas_call | solution.py:389
  251.6 1.0 copy.9

commit v3 on v2

--- a/solution.py
+++ b/solution.py
@@ -12,6 +12,7 @@
 COLS = 256
 AG_CHUNKS = 2
 SIB_SLOTS = 4
+PACK = 2
 MESH = pl.DeviceIdType.MESH
 BF16 = jnp.bfloat16
 F32 = jnp.float32
@@ -102,8 +103,9 @@
     for dev in (side[0], side[1], sib):
         pl.semaphore_signal(barrier, inc=1, device_id={'ep': dev}, device_id_type=MESH)
     local = (pltpu.make_async_copy(ids_in, raw.at[0], local_sem.at[0]), pltpu.make_async_copy(slots_in, raw.at[1], local_sem.at[1]),
-             pltpu.make_async_copy(gates_in, meta.at[me, pl.ds(top_k, top_k)], local_sem.at[2]), pltpu.make_async_copy(tok_in, tok.at[me], local_sem.at[3]))
-    for copy in local:
+             pltpu.make_async_copy(gates_in, meta.at[me, pl.ds(top_k, top_k)], local_sem.at[2]))
+    bands = [pltpu.make_async_copy(tok_in.at[part_rows(way, 0, ck)], tok.at[me, part_rows(way, 0, ck)], local_sem.at[3 + ck * 2 + way]) for ck in range(AG_CHUNKS) for way in range(2)]
+    for copy in local + tuple(bands):
         copy.start()
     for copy in local[:2]:
         copy.wait()
@@ -111,33 +113,33 @@
     meta[me, pl.ds(0, top_k), :] = jnp.where(slot_ids >= 0, raw[0] * cap + slot_ids - me * cap, -1).astype(F32)
     for idx in range(0, n_w, 2):
         load_up(jnp.int32(idx), idx, begin)
-    for copy in local[2:]:
-        copy.wait()
     pl.semaphore_wait(barrier, 3)
 
     own_tok = lambda core_num: to_sib(tok.at[place(chip, core_num)], own_s.at[0], own_r.at[0])
     own_meta = lambda core_num: to_sib(meta.at[place(chip, core_num)], own_s.at[1], own_r.at[1])
-    for way in range(2):
-        ag_meta(way, 1, False)[0].start()
     for ck in range(AG_CHUNKS):
         for way in range(2):
+            bands[ck * 2 + way].wait()
             ag(way, 0, 1, ck, False)[0].start()
+        if ck == 0:
+            local[2].wait()
+            for way in range(2):
+                ag_meta(way, 1, False)[0].start()
     own_meta(core).start()
     own_tok(core).start()
     obuf[...] = jnp.zeros_like(obuf)
     for hop in range(1, far + 1):
-        for way in range(2):
-            if hop <= meta_hops[way]:
-                ag_meta(way, hop, True)[0].wait_recv()
-                if hop < meta_hops[way]:
-                    ag_meta(way, hop + 1, False)[0].start()
-                sib_meta(way, hop, core).start()
         for ck in range(AG_CHUNKS):
             for way in range(2):
                 ag(way, 0, hop, ck, True)[0].wait_recv()
                 if hop < far:
                     ag(way, 0, hop + 1, ck, False)[0].start()
                 sib_msg(way, 0, hop, ck, core).start()
+                if ck == 0 and hop <= meta_hops[way]:
+                    ag_meta(way, hop, True)[0].wait_recv()
+                    if hop < meta_hops[way]:
+                        ag_meta(way, hop + 1, False)[0].start()
+                    sib_meta(way, hop, core).start()
         if hop == far - 1:
             for ck in range(AG_CHUNKS):
                 for way in range(2):
@@ -159,6 +161,16 @@
         return pltpu.make_async_remote_copy(ring.at[way, slot, d], ring.at[way, slot + 1, d], rs_s.at[way, slot, d], rs_r.at[way, slot + 1, d], device_id={'ep': side[way]}, device_id_type=MESH)
 
     def rs_wait(way, slot, d):
+        @pl.when(d % PACK == 0)
+        def _():
+            rs_arrived(way, slot, d // PACK)
+
+    def rs_send(way, slot, d):
+        @pl.when(d % PACK == PACK - 1)
+        def _():
+            rs(way, slot, d // PACK).start()
+
+    def rs_arrived(way, slot, d):
         pltpu.make_async_remote_copy(ring.at[way, slot, d], ring.at[way, slot, d], rs_s.at[way, slot, d], rs_r.at[way, slot, d], device_id={'ep': side[way]}, device_id_type=MESH).wait_recv()
 
     lane_rows = (pl.ds(0, half), pl.ds(half, half))
@@ -242,12 +254,12 @@
                     rs_wait(way, a_slot + far, d)
                     rs_wait(way, b_slot + far - 1, d)
                 for r in range(2):
-                    total = mine(0, r) + ring[r, a_slot + far, d] + ring[1 - r, b_slot + far - 1, d]
+                    total = mine(0, r) + ring[r, a_slot + far, d // PACK, d % PACK] + ring[1 - r, b_slot + far - 1, d // PACK, d % PACK]
                     out[lane_rows[r], pl.ds(pl.multiple_of(d * COLS, COLS), COLS)] = total.astype(BF16)
             elif width == 1:
                 for way in range(2):
-                    ring[way, a_slot, d] = mine(0, way)
-                    rs(way, a_slot, d).start()
+                    ring[way, a_slot, d // PACK, d % PACK] = mine(0, way)
+                    rs_send(way, a_slot, d)
             else:
                 b_now = b_slot + far - 1 - dist
                 a_now = a_slot + far - dist
@@ -255,19 +267,19 @@
                 @pl.when(dist == far - 1)
                 def _():
                     for way in range(2):
-                        ring[way, b_slot, d] = mine(way, 1 - way)
+                        ring[way, b_slot, d // PACK, d % PACK] = mine(way, 1 - way)
 
                 @pl.when(dist != far - 1)
                 def _():
                     for way in range(2):
                         rs_wait(way, b_now, d)
-                        ring[way, b_now, d] += mine(way, 1 - way)
+                        ring[way, b_now, d // PACK, d % PACK] += mine(way, 1 - way)
                 for way in range(2):
-                    rs(way, b_now, d).start()
+                    rs_send(way, b_now, d)
                 for way in range(2):
                     rs_wait(way, a_now, d)
-                    ring[way, a_now, d] += mine(way, way)
-                    rs(way, a_now, d).start()
+                    ring[way, a_now, d // PACK, d % PACK] += mine(way, way)
+                    rs_send(way, a_now, d)
 
             @pl.when(count < total_chunks - SIB_SLOTS)
             def _():
@@ -370,7 +382,7 @@
             for slot in list(range(a_slot, a_slot + far)) + list(range(b_slot, b_slot + far - 1)):
                 rs(way, slot, d).wait_send()
             return carry
-        lax.fori_loop(0, n_d, drain, 0)
+        lax.fori_loop(0, n_d // PACK, drain, 0)
 
 
 def group_layer(n, tokens, ids, gates, slot_ids, w_gate, w_up, w_down, cap):
@@ -395,7 +407,7 @@
             pltpu.VMEM((n, rows, d_model), BF16),
             pltpu.VMEM((n, 2 * top_k, rows), F32),
             pltpu.VMEM((2, top_k, rows), jnp.int32),
-            pltpu.VMEM((2, 2 * far + 1, n_d, rows // 2, COLS), F32),
+            pltpu.VMEM((2, 2 * far + 1, n_d // PACK, PACK, rows // 2, COLS), F32),
             pltpu.VMEM((SIB_SLOTS, 2, rows, COLS), F32),
             pltpu.VMEM((2, 2, rows, COLS), F32),
             pltpu.VMEM((2, 2, rows, COLS), F32),
@@ -405,11 +417,11 @@
             pltpu.VMEM((4, 3 * slots, COLS), BF16),
             pltpu.VMEM((4, rows, slots), BF16),
             pltpu.VMEM((n_exp, 4 * cap, 128), F32),
-            dma((4,)), dma((n_w, 2)),
+            dma((3 + 2 * AG_CHUNKS,)), dma((n_w, 2)),
             dma(ag_shape), dma(ag_shape), dma((2, far)), dma((2, far)),
             dma(ag_shape), dma(ag_shape), dma((2, far)), dma((2, far)),
             dma((2,)), dma((2,)),
-            dma((2, 2 * far + 1, n_d)), dma((2, 2 * far + 1, n_d)),
+            dma((2, 2 * far + 1, n_d // PACK)), dma((2, 2 * far + 1, n_d // PACK)),
             dma((2,)), dma((SIB_SLOTS,)),
             pltpu.SemaphoreType.REGULAR,
         ],

time: 253 us -> 252 us (level)
  no operation moved by 1% of the time
where the time goes in v3:
time: 252 us
  Pallas kernels  251 us (100%)
    pallas_call x1, Pallas kernels, group_layer(): pl.pallas_call(functools.partial(moe_kernel, (n, cap, spad, n_w)), out_sh...  251 us

profile of v3, /device:TPU:21, one launch (start us, length us, event | category | flops | bytes accessed | tf_op | source)
XLA Modules:
  0.0 252.3 jit_solution(251558486211942063)
XLA Ops:
  0.0 251.3 %shard_map.73 = bf16[256,2048]{1,0:T(8,128)(2,1)S(1)} custom-call(bf16[256,2048]{1,0:T(8,128)(2,1)} %tok_in.1, s32[8,256]{1,0:T(8,128)} %bitcast.3, f32[8,256]{1,0:T(8,128)} %bitcast.4, s32[8,256]{1,0:T(8,128)} %bitcast.5, bf16[4,2048,1024]{2,1,0:T(8,128)(2,1)} %wg.1, bf16[4,2048,1024]{2,1,0:T(8,128)(2,1)} %wu.1, bf16[4,1024,2048]{2,1,0:T(8,128)(2,1)} %wd.1), custom_call_target="tpu_custom_call" | custom-call | tf_op jit(solution)/shard_map/pallas_call | solution.py:401
  251.3 1.0 copy.9

commit v4 on v3

--- a/solution.py
+++ b/solution.py
@@ -19,7 +19,7 @@
 
 
 def moe_kernel(cfg, tok_in, ids_in, gates_in, slots_in, wg, wu, wd, out,
-               tok, meta, raw, ring, sib_in, sib_out, own, wbuf, xbuf, hbuf, obuf, ptbuf, sgbuf,
+               tok, meta, raw, ring, sib_in, sib_out, own, wbuf, xbuf, hbuf, obuf, ptbuf, pbuf, sgbuf,
                local_sem, w_sem, ag_s, ag_r, agm_s, agm_r, sb_s, sb_r, sbm_s, sbm_r, own_s, own_r,
                rs_s, rs_r, ss_s, ss_r, credit):
     n, cap, spad, n_w = cfg
@@ -175,7 +175,7 @@
 
     lane_rows = (pl.ds(0, half), pl.ds(half, half))
 
-    def phase(dist, order, shards, last=False, events=False):
+    def phase(dist, order, shards, arrive, last=False, events=False):
         width = shards // 2
         m_rows = shards * cap
 
@@ -184,7 +184,7 @@
             step = dist if width == 1 else dist * (1 - 2 * which)
             return place(chip + step, jnp.where(num < width, core, other))
 
-        def gather(num, carry):
+        def masks(num, carry):
             shard = shard_place(num)
             base = (me * n_exp * cap).astype(F32)
             row_num = lax.broadcasted_iota(jnp.int32, (slots, rows), 0)
@@ -203,13 +203,21 @@
             for e in range(n_exp):
                 sgbuf[e, pl.ds(first, cap), :] = slot_gate[e * spad:e * spad + cap]
             ptbuf[num] = hot.T.astype(BF16)
-            pick = hot.astype(BF16)
+            pbuf[num] = hot.astype(BF16)
+            return carry
+
+        def gather(num, carry):
+            shard = shard_place(num)
+            first = pl.multiple_of(num * cap, 16)
+            pick = pbuf[num]
             for c in range(d_model // COLS):
                 got = jnp.dot(pick, tok[shard, :, pl.ds(c * COLS, COLS)], preferred_element_type=F32).astype(BF16)
                 for e in range(n_exp):
                     xbuf[e, pl.ds(first, cap), pl.ds(c * COLS, COLS)] = got[e * spad:e * spad + cap]
             return carry
 
+        lax.fori_loop(0, shards, masks, 0)
+        arrive()
         lax.fori_loop(0, shards, gather, 0)
 
         def up_step(step, carry):
@@ -332,10 +340,9 @@
             def _():
                 close(d - 1)
             if events:
-                for k in range(2):
-                    @pl.when(d == (k + 1) * n_d // 2 - 1)
-                    def _():
-                        second_half_event(n_events - 2 + k)
+                @pl.when(d == n_d // 2 - 1)
+                def _():
+                    second_half_event(n_events - 2)
             return carry
 
         lax.fori_loop(0, n_d, down_step, 0)
@@ -343,27 +350,44 @@
         for d in range(n_d - 2, n_d):
             sib_share(d).wait_send()
 
+    def far_rows():
+        for way in range(2):
+            for ck in range(AG_CHUNKS):
+                sib_msg(way, 0, far, ck, other).wait_recv()
+
     for way in range(2):
         if far <= meta_hops[way]:
             sib_meta(way, far, other).wait_recv()
-        for ck in range(AG_CHUNKS):
-            sib_msg(way, 0, far, ck, other).wait_recv()
-    phase(far, 0, 2, events=True)
+    phase(far, 0, 2, far_rows, events=True)
 
     def middle(order, carry):
         dist = far - order
+
+        def rows_of():
+            @pl.when(order == 1)
+            def _():
+                second_half_event(n_events - 1)
+            for way in range(2):
+                for kind in range(2):
+                    for ck in range(AG_CHUNKS):
+                        sib_msg(way, kind, dist, ck, other).wait_recv()
+
         for way in range(2):
             sib_meta(way, dist, other).wait_recv()
-            for kind in range(2):
-                for ck in range(AG_CHUNKS):
-                    sib_msg(way, kind, dist, ck, other).wait_recv()
-        phase(dist, order, 4)
+        phase(dist, order, 4, rows_of)
         return carry
 
     lax.fori_loop(1, far, middle, 0)
     own_meta(other).wait_recv()
     own_tok(other).wait_recv()
-    phase(0, far, 2, last=True)
+
+    def drained(slots):
+        def drain(d, carry):
+            for way in range(2):
+                for slot in slots:
+                    rs(way, slot, d).wait_send()
+            return carry
+        lax.fori_loop(0, n_d // PACK, drain, 0)
 
     own_meta(core).wait_send()
     own_tok(core).wait_send()
@@ -377,12 +401,9 @@
                     for ck in range(AG_CHUNKS):
                         ag(way, kind, hop, ck, False)[0].wait_send()
                         sib_msg(way, kind, hop, ck, core).wait_send()
-
-        def drain(d, carry):
-            for slot in list(range(a_slot, a_slot + far)) + list(range(b_slot, b_slot + far - 1)):
-                rs(way, slot, d).wait_send()
-            return carry
-        lax.fori_loop(0, n_d // PACK, drain, 0)
+    drained(list(range(a_slot, a_slot + far - 1)) + list(range(b_slot, b_slot + far - 2)))
+    phase(0, far, 2, lambda: None, last=True)
+    drained([a_slot + far - 1, b_slot + far - 2])
 
 
 def group_layer(n, tokens, ids, gates, slot_ids, w_gate, w_up, w_down, cap):
@@ -394,7 +415,7 @@
     slots = n_exp * spad
     n_d = d_model // COLS
     loads = 2 * n_exp * d_ff // COLS + n_d * n_exp // 2
-    n_w = 8 if loads % 8 == 0 else 4
+    n_w = next(k for k in (12, 8, 6, 4) if loads % k == 0 and k <= n_d * n_exp // 2)
     any_spec = pl.BlockSpec(memory_space=pl.ANY)
     dma = pltpu.SemaphoreType.DMA
     ag_shape = (2, 2, far, AG_CHUNKS)
@@ -416,6 +437,7 @@
             pltpu.VMEM((n_exp, 4 * cap, d_ff), BF16),
             pltpu.VMEM((4, 3 * slots, COLS), BF16),
             pltpu.VMEM((4, rows, slots), BF16),
+            pltpu.VMEM((4, slots, rows), BF16),
             pltpu.VMEM((n_exp, 4 * cap, 128), F32),
             dma((3 + 2 * AG_CHUNKS,)), dma((n_w, 2)),
             dma(ag_shape), dma(ag_shape), dma((2, far)), dma((2, far)),
@@ -425,7 +447,7 @@
             dma((2,)), dma((SIB_SLOTS,)),
             pltpu.SemaphoreType.REGULAR,
         ],
-        compiler_params=pltpu.CompilerParams(collective_id=0, has_side_effects=True, vmem_limit_bytes=58 << 20),
+        compiler_params=pltpu.CompilerParams(collective_id=0, has_side_effects=True, vmem_limit_bytes=61 << 20),
     )(tokens, ids, gates, slot_ids, w_gate, w_up, w_down)
 
 

time: 252 us -> 253 us (level)
  no operation moved by 1% of the time
where the time goes in v4:
time: 253 us
  Pallas kernels  252 us (100%)
    pallas_call x1, Pallas kernels, group_layer(): pl.pallas_call(functools.partial(moe_kernel, (n, cap, spad, n_w)), out_sh...  252 us

profile of v4, /device:TPU:21, one launch (start us, length us, event | category | flops | bytes accessed | tf_op | source)
XLA Modules:
  0.0 252.8 jit_solution(16583860680939513486)
XLA Ops:
  0.0 251.8 %shard_map.73 = bf16[256,2048]{1,0:T(8,128)(2,1)S(1)} custom-call(bf16[256,2048]{1,0:T(8,128)(2,1)} %tok_in.1, s32[8,256]{1,0:T(8,128)} %bitcast.3, f32[8,256]{1,0:T(8,128)} %bitcast.4, s32[8,256]{1,0:T(8,128)} %bitcast.5, bf16[4,2048,1024]{2,1,0:T(8,128)(2,1)} %wg.1, bf16[4,2048,1024]{2,1,0:T(8,128)(2,1)} %wu.1, bf16[4,1024,2048]{2,1,0:T(8,128)(2,1)} %wd.1), custom_call_target="tpu_custom_call" | custom-call | tf_op jit(solution)/shard_map/pallas_call | solution.py:422
  251.9 1.0 copy.9

commit v5 on v4

--- a/solution.py
+++ b/solution.py
@@ -111,8 +111,6 @@
         copy.wait()
     slot_ids = raw[1]
     meta[me, pl.ds(0, top_k), :] = jnp.where(slot_ids >= 0, raw[0] * cap + slot_ids - me * cap, -1).astype(F32)
-    for idx in range(0, n_w, 2):
-        load_up(jnp.int32(idx), idx, begin)
     pl.semaphore_wait(barrier, 3)
 
     own_tok = lambda core_num: to_sib(tok.at[place(chip, core_num)], own_s.at[0], own_r.at[0])
@@ -125,8 +123,8 @@
             local[2].wait()
             for way in range(2):
                 ag_meta(way, 1, False)[0].start()
-    own_meta(core).start()
-    own_tok(core).start()
+    for idx in range(0, n_w, 2):
+        load_up(jnp.int32(idx), idx, begin)
     obuf[...] = jnp.zeros_like(obuf)
     for hop in range(1, far + 1):
         for ck in range(AG_CHUNKS):
@@ -141,6 +139,8 @@
                         ag_meta(way, hop + 1, False)[0].start()
                     sib_meta(way, hop, core).start()
         if hop == far - 1:
+            own_meta(core).start()
+            own_tok(core).start()
             for ck in range(AG_CHUNKS):
                 for way in range(2):
                     ag(way, 1, 1, ck, False)[0].start()
@@ -415,7 +415,7 @@
     slots = n_exp * spad
     n_d = d_model // COLS
     loads = 2 * n_exp * d_ff // COLS + n_d * n_exp // 2
-    n_w = next(k for k in (12, 8, 6, 4) if loads % k == 0 and k <= n_d * n_exp // 2)
+    n_w = next(k for k in (8, 6, 4) if loads % k == 0 and k <= n_d * n_exp // 2)
     any_spec = pl.BlockSpec(memory_space=pl.ANY)
     dma = pltpu.SemaphoreType.DMA
     ag_shape = (2, 2, far, AG_CHUNKS)
@@ -447,7 +447,7 @@
             dma((2,)), dma((SIB_SLOTS,)),
             pltpu.SemaphoreType.REGULAR,
         ],
-        compiler_params=pltpu.CompilerParams(collective_id=0, has_side_effects=True, vmem_limit_bytes=61 << 20),
+        compiler_params=pltpu.CompilerParams(collective_id=0, has_side_effects=True, vmem_limit_bytes=58 << 20),
     )(tokens, ids, gates, slot_ids, w_gate, w_up, w_down)
 
 

time: 253 us -> 253 us (level)
  no operation moved by 1% of the time
where the time goes in v5:
time: 253 us
  Pallas kernels  252 us (100%)
    pallas_call x1, Pallas kernels, group_layer(): pl.pallas_call(functools.partial(moe_kernel, (n, cap, spad, n_w)), out_sh...  252 us

profile of v5, /device:TPU:21, one launch (start us, length us, event | category | flops | bytes accessed | tf_op | source)
XLA Modules:
  0.0 252.9 jit_solution(12887686801799924543)
XLA Ops:
  0.0 251.9 %shard_map.73 = bf16[256,2048]{1,0:T(8,128)(2,1)S(1)} custom-call(bf16[256,2048]{1,0:T(8,128)(2,1)} %tok_in.1, s32[8,256]{1,0:T(8,128)} %bitcast.3, f32[8,256]{1,0:T(8,128)} %bitcast.4, s32[8,256]{1,0:T(8,128)} %bitcast.5, bf16[4,2048,1024]{2,1,0:T(8,128)(2,1)} %wg.1, bf16[4,2048,1024]{2,1,0:T(8,128)(2,1)} %wu.1, bf16[4,1024,2048]{2,1,0:T(8,128)(2,1)} %wd.1), custom_call_target="tpu_custom_call" | custom-call | tf_op jit(solution)/shard_map/pallas_call | solution.py:422
  251.9 1.0 copy.9

commit v6 on v3

--- a/solution.py
+++ b/solution.py
@@ -20,7 +20,7 @@
 
 def moe_kernel(cfg, tok_in, ids_in, gates_in, slots_in, wg, wu, wd, out,
                tok, meta, raw, ring, sib_in, sib_out, own, wbuf, xbuf, hbuf, obuf, ptbuf, sgbuf,
-               local_sem, w_sem, ag_s, ag_r, agm_s, agm_r, sb_s, sb_r, sbm_s, sbm_r, own_s, own_r,
+               local_sem, w_sem, ag_s, ag_r, agm_s, agm_r, sb_s, sb_r, sbm_s, sbm_r, own_s, own_r, guest_s, guest_r,
                rs_s, rs_r, ss_s, ss_r, credit):
     n, cap, spad, n_w = cfg
     rows, d_model = tok_in.shape
@@ -98,6 +98,28 @@
         return to_sib(meta.at[place(chip - sign[way] * hop, core_num)], sbm_s.at[way, hop - 1], sbm_r.at[way, hop - 1])
 
     meta_hops = (far, far - 1)
+    swap_ck = AG_CHUNKS - 1
+
+    def split_rows(way, num):
+        return pl.ds((0 if way == 0 else half) + swap_ck * piece + num * (piece // 2), piece // 2)
+
+    def stay(way, arriving):
+        origin = place(chip - sign[way] * (far if arriving else far - 1), 1)
+        view = tok.at[origin, split_rows(way, 0)]
+        return pltpu.make_async_remote_copy(view, view, ag_s.at[way, 0, far - 1, swap_ck], ag_r.at[way, 0, far - 1, swap_ck], device_id={'ep': side[way]}, device_id_type=MESH)
+
+    def stay_sib(way):
+        origin = place(chip - sign[way] * far, 1)
+        return to_sib(tok.at[origin, split_rows(way, 0)], sb_s.at[way, 0, far - 1, swap_ck], sb_r.at[way, 0, far - 1, swap_ck])
+
+    def guest(way, arriving):
+        origin = place(chip - sign[way] * (far if arriving else far - 1), 1)
+        view = tok.at[origin, split_rows(way, 1)]
+        return pltpu.make_async_remote_copy(view, view, guest_s.at[way, 0], guest_r.at[way, 0], device_id={'ep': side[way]}, device_id_type=MESH)
+
+    def guest_sib(way):
+        origin = place(chip - sign[way] * far, 1)
+        return to_sib(tok.at[origin, split_rows(way, 1)], guest_s.at[way, 1], guest_r.at[way, 1])
 
     barrier = pltpu.get_barrier_semaphore()
     for dev in (side[0], side[1], sib):
@@ -107,12 +129,6 @@
     bands = [pltpu.make_async_copy(tok_in.at[part_rows(way, 0, ck)], tok.at[me, part_rows(way, 0, ck)], local_sem.at[3 + ck * 2 + way]) for ck in range(AG_CHUNKS) for way in range(2)]
     for copy in local + tuple(bands):
         copy.start()
-    for copy in local[:2]:
-        copy.wait()
-    slot_ids = raw[1]
-    meta[me, pl.ds(0, top_k), :] = jnp.where(slot_ids >= 0, raw[0] * cap + slot_ids - me * cap, -1).astype(F32)
-    for idx in range(0, n_w, 2):
-        load_up(jnp.int32(idx), idx, begin)
     pl.semaphore_wait(barrier, 3)
 
     own_tok = lambda core_num: to_sib(tok.at[place(chip, core_num)], own_s.at[0], own_r.at[0])
@@ -122,24 +138,56 @@
             bands[ck * 2 + way].wait()
             ag(way, 0, 1, ck, False)[0].start()
         if ck == 0:
-            local[2].wait()
-            for way in range(2):
-                ag_meta(way, 1, False)[0].start()
+            for copy in local:
+                copy.wait()
+            slot_ids = raw[1]
+            meta[me, pl.ds(0, top_k), :] = jnp.where(slot_ids >= 0, raw[0] * cap + slot_ids - me * cap, -1).astype(F32)
+    for way in range(2):
+        ag_meta(way, 1, False)[0].start()
     own_meta(core).start()
     own_tok(core).start()
+    for idx in range(0, n_w, 2):
+        load_up(jnp.int32(idx), idx, begin)
     obuf[...] = jnp.zeros_like(obuf)
     for hop in range(1, far + 1):
         for ck in range(AG_CHUNKS):
             for way in range(2):
+                if hop == far and ck == swap_ck:
+                    @pl.when(core == 0)
+                    def _():
+                        ag(way, 0, hop, ck, True)[0].wait_recv()
+                        sib_msg(way, 0, hop, ck, core).start()
+                        guest(way, True).wait_recv()
+                        guest_sib(way).start()
+
+                    @pl.when(core == 1)
+                    def _():
+                        stay(way, True).wait_recv()
+                        stay_sib(way).start()
+                    continue
                 ag(way, 0, hop, ck, True)[0].wait_recv()
+                if hop + 1 == far and ck == swap_ck:
+                    sib_msg(way, 0, hop, ck, core).start()
+
+                    @pl.when(core == 0)
+                    def _():
+                        ag(way, 0, hop + 1, ck, False)[0].start()
+                        sib_msg(way, 0, hop, ck, other).wait_recv()
+                        guest(way, False).start()
+
+                    @pl.when(core == 1)
+                    def _():
+                        stay(way, False).start()
+                    continue
                 if hop < far:
                     ag(way, 0, hop + 1, ck, False)[0].start()
                 sib_msg(way, 0, hop, ck, core).start()
-                if ck == 0 and hop <= meta_hops[way]:
-                    ag_meta(way, hop, True)[0].wait_recv()
-                    if hop < meta_hops[way]:
-                        ag_meta(way, hop + 1, False)[0].start()
-                    sib_meta(way, hop, core).start()
+        for way in range(2):
+            if hop <= meta_hops[way]:
+                ag_meta(way, hop, True)[0].wait_recv()
+                if hop < meta_hops[way]:
+                    ag_meta(way, hop + 1, False)[0].start()
+                sib_meta(way, hop, core).start()
         if hop == far - 1:
             for ck in range(AG_CHUNKS):
                 for way in range(2):
@@ -347,7 +395,17 @@
         if far <= meta_hops[way]:
             sib_meta(way, far, other).wait_recv()
         for ck in range(AG_CHUNKS):
-            sib_msg(way, 0, far, ck, other).wait_recv()
+            if ck != swap_ck:
+                sib_msg(way, 0, far, ck, other).wait_recv()
+
+        @pl.when(core == 0)
+        def _():
+            stay_sib(way).wait_recv()
+
+        @pl.when(core == 1)
+        def _():
+            sib_msg(way, 0, far, swap_ck, other).wait_recv()
+            guest_sib(way).wait_recv()
     phase(far, 0, 2, events=True)
 
     def middle(order, carry):
@@ -356,7 +414,12 @@
             sib_meta(way, dist, other).wait_recv()
             for kind in range(2):
                 for ck in range(AG_CHUNKS):
-                    sib_msg(way, kind, dist, ck, other).wait_recv()
+                    if kind == 0 and ck == swap_ck:
+                        @pl.when((core == 1) | (dist != far - 1))
+                        def _():
+                            sib_msg(way, kind, dist, ck, other).wait_recv()
+                    else:
+                        sib_msg(way, kind, dist, ck, other).wait_recv()
         phase(dist, order, 4)
         return carry
 
@@ -375,8 +438,21 @@
             for kind in range(2):
                 if hop <= far - kind:
                     for ck in range(AG_CHUNKS):
-                        ag(way, kind, hop, ck, False)[0].wait_send()
-                        sib_msg(way, kind, hop, ck, core).wait_send()
+                        if kind == 0 and hop == far and ck == swap_ck:
+                            @pl.when(core == 0)
+                            def _():
+                                ag(way, kind, hop, ck, False)[0].wait_send()
+                                sib_msg(way, kind, hop, ck, core).wait_send()
+                                guest(way, False).wait_send()
+                                guest_sib(way).wait_send()
+
+                            @pl.when(core == 1)
+                            def _():
+                                stay(way, False).wait_send()
+                                stay_sib(way).wait_send()
+                        else:
+                            ag(way, kind, hop, ck, False)[0].wait_send()
+                            sib_msg(way, kind, hop, ck, core).wait_send()
 
         def drain(d, carry):
             for slot in list(range(a_slot, a_slot + far)) + list(range(b_slot, b_slot + far - 1)):
@@ -420,7 +496,7 @@
             dma((3 + 2 * AG_CHUNKS,)), dma((n_w, 2)),
             dma(ag_shape), dma(ag_shape), dma((2, far)), dma((2, far)),
             dma(ag_shape), dma(ag_shape), dma((2, far)), dma((2, far)),
-            dma((2,)), dma((2,)),
+            dma((2,)), dma((2,)), dma((2, 2)), dma((2, 2)),
             dma((2, 2 * far + 1, n_d // PACK)), dma((2, 2 * far + 1, n_d // PACK)),
             dma((2,)), dma((SIB_SLOTS,)),
             pltpu.SemaphoreType.REGULAR,

time: 252 us -> 252 us (level)
  no operation moved by 1% of the time
where the time goes in v6:
time: 252 us
  Pallas kernels  251 us (100%)
    pallas_call x1, Pallas kernels, group_layer(): pl.pallas_call(functools.partial(moe_kernel, (n, cap, spad, n_w)), out_sh...  251 us

profile of v6, /device:TPU:21, one launch (start us, length us, event | category | flops | bytes accessed | tf_op | source)
XLA Modules:
  0.0 251.7 jit_solution(3274285564705145949)
XLA Ops:
  0.0 250.8 %shard_map.73 = bf16[256,2048]{1,0:T(8,128)(2,1)S(1)} custom-call(bf16[256,2048]{1,0:T(8,128)(2,1)} %tok_in.1, s32[8,256]{1,0:T(8,128)} %bitcast.3, f32[8,256]{1,0:T(8,128)} %bitcast.4, s32[8,256]{1,0:T(8,128)} %bitcast.5, bf16[4,2048,1024]{2,1,0:T(8,128)(2,1)} %wg.1, bf16[4,2048,1024]{2,1,0:T(8,128)(2,1)} %wu.1, bf16[4,1024,2048]{2,1,0:T(8,128)(2,1)} %wd.1), custom_call_target="tpu_custom_call" | custom-call | tf_op jit(solution)/shard_map/pallas_call | solution.py:477
  250.8 1.0 copy.9

commit v7 on v3

--- a/solution.py
+++ b/solution.py
@@ -107,12 +107,6 @@
     bands = [pltpu.make_async_copy(tok_in.at[part_rows(way, 0, ck)], tok.at[me, part_rows(way, 0, ck)], local_sem.at[3 + ck * 2 + way]) for ck in range(AG_CHUNKS) for way in range(2)]
     for copy in local + tuple(bands):
         copy.start()
-    for copy in local[:2]:
-        copy.wait()
-    slot_ids = raw[1]
-    meta[me, pl.ds(0, top_k), :] = jnp.where(slot_ids >= 0, raw[0] * cap + slot_ids - me * cap, -1).astype(F32)
-    for idx in range(0, n_w, 2):
-        load_up(jnp.int32(idx), idx, begin)
     pl.semaphore_wait(barrier, 3)
 
     own_tok = lambda core_num: to_sib(tok.at[place(chip, core_num)], own_s.at[0], own_r.at[0])
@@ -122,11 +116,16 @@
             bands[ck * 2 + way].wait()
             ag(way, 0, 1, ck, False)[0].start()
         if ck == 0:
-            local[2].wait()
-            for way in range(2):
-                ag_meta(way, 1, False)[0].start()
+            for copy in local:
+                copy.wait()
+            slot_ids = raw[1]
+            meta[me, pl.ds(0, top_k), :] = jnp.where(slot_ids >= 0, raw[0] * cap + slot_ids - me * cap, -1).astype(F32)
+    for way in range(2):
+        ag_meta(way, 1, False)[0].start()
     own_meta(core).start()
     own_tok(core).start()
+    for idx in range(0, n_w, 2):
+        load_up(jnp.int32(idx), idx, begin)
     obuf[...] = jnp.zeros_like(obuf)
     for hop in range(1, far + 1):
         for ck in range(AG_CHUNKS):
@@ -135,11 +134,12 @@
                 if hop < far:
                     ag(way, 0, hop + 1, ck, False)[0].start()
                 sib_msg(way, 0, hop, ck, core).start()
-                if ck == 0 and hop <= meta_hops[way]:
-                    ag_meta(way, hop, True)[0].wait_recv()
-                    if hop < meta_hops[way]:
-                        ag_meta(way, hop + 1, False)[0].start()
-                    sib_meta(way, hop, core).start()
+        for way in range(2):
+            if hop <= meta_hops[way]:
+                ag_meta(way, hop, True)[0].wait_recv()
+                if hop < meta_hops[way]:
+                    ag_meta(way, hop + 1, False)[0].start()
+                sib_meta(way, hop, core).start()
         if hop == far - 1:
             for ck in range(AG_CHUNKS):
                 for way in range(2):
@@ -156,6 +156,10 @@
             sib_msg(way, 1, hop, ck, core).start()
 
     n_events = (far - 1) * AG_CHUNKS
+    n_up = n_exp * n_f
+    up_events = [(3 * n_up) // 8 - 1, (3 * n_up) // 4 - 1]
+    late = n_events - len(up_events)
+    down_events = [k * n_d // late for k in range(late)]
 
     def rs(way, slot, d):
         return pltpu.make_async_remote_copy(ring.at[way, slot, d], ring.at[way, slot + 1, d], rs_s.at[way, slot, d], rs_r.at[way, slot + 1, d], device_id={'ep': side[way]}, device_id_type=MESH)
@@ -231,11 +235,10 @@
                 for k in range(2):
                     load_down(idx + n_w + k - up_loads, slot + k, begin)
             if events:
-                every = max(n_exp * n_f // max(n_events - 2, 1), 1)
-
-                @pl.when((step % every == every - 1) & (step // every < n_events - 2))
-                def _():
-                    second_half_event(step // every)
+                for k, at in enumerate(up_events):
+                    @pl.when(step == at)
+                    def _():
+                        second_half_event(k)
             return carry
 
         lax.fori_loop(0, n_exp * n_f, up_step, 0)
@@ -332,10 +335,10 @@
             def _():
                 close(d - 1)
             if events:
-                for k in range(2):
-                    @pl.when(d == (k + 1) * n_d // 2 - 1)
+                for k, at in enumerate(down_events):
+                    @pl.when(d == at)
                     def _():
-                        second_half_event(n_events - 2 + k)
+                        second_half_event(len(up_events) + k)
             return carry
 
         lax.fori_loop(0, n_d, down_step, 0)

time: 252 us -> 258 us (1.024)
  Pallas kernels: 251 us -> 257 us
    pallas_call x1, Pallas kernels: 251 us -> 257 us  [group_layer(): pl.pallas_call(functools.partial(moe_kernel, (n, cap, spad, n_w)), out_sh...]
where the time goes in v7:
time: 258 us
  Pallas kernels  257 us (100%)
    pallas_call x1, Pallas kernels, group_layer(): pl.pallas_call(functools.partial(moe_kernel, (n, cap, spad, n_w)), out_sh...  257 us

profile of v7, /device:TPU:21, one launch (start us, length us, event | category | flops | bytes accessed | tf_op | source)
XLA Modules:
  0.0 258.0 jit_solution(10140183169708557419)
XLA Ops:
  0.0 257.1 %shard_map.73 = bf16[256,2048]{1,0:T(8,128)(2,1)S(1)} custom-call(bf16[256,2048]{1,0:T(8,128)(2,1)} %tok_in.1, s32[8,256]{1,0:T(8,128)} %bitcast.3, f32[8,256]{1,0:T(8,128)} %bitcast.4, s32[8,256]{1,0:T(8,128)} %bitcast.5, bf16[4,2048,1024]{2,1,0:T(8,128)(2,1)} %wg.1, bf16[4,2048,1024]{2,1,0:T(8,128)(2,1)} %wu.1, bf16[4,1024,2048]{2,1,0:T(8,128)(2,1)} %wd.1), custom_call_target="tpu_custom_call" | custom-call | tf_op jit(solution)/shard_map/pallas_call | solution.py:404
  257.1 1.0 copy.9

commit v8 on v7

--- a/solution.py
+++ b/solution.py
@@ -157,9 +157,8 @@
 
     n_events = (far - 1) * AG_CHUNKS
     n_up = n_exp * n_f
-    up_events = [(3 * n_up) // 8 - 1, (3 * n_up) // 4 - 1]
-    late = n_events - len(up_events)
-    down_events = [k * n_d // late for k in range(late)]
+    up_events = [(k + 1) * n_up // (n_events - 2) - 1 for k in range(n_events - 2)]
+    down_events = [n_d // 2 - 1, n_d - 1]
 
     def rs(way, slot, d):
         return pltpu.make_async_remote_copy(ring.at[way, slot, d], ring.at[way, slot + 1, d], rs_s.at[way, slot, d], rs_r.at[way, slot + 1, d], device_id={'ep': side[way]}, device_id_type=MESH)
@@ -397,7 +396,7 @@
     slots = n_exp * spad
     n_d = d_model // COLS
     loads = 2 * n_exp * d_ff // COLS + n_d * n_exp // 2
-    n_w = 8 if loads % 8 == 0 else 4
+    n_w = next(k for k in (12, 8, 6, 4) if loads % k == 0 and k <= n_d * n_exp // 2)
     any_spec = pl.BlockSpec(memory_space=pl.ANY)
     dma = pltpu.SemaphoreType.DMA
     ag_shape = (2, 2, far, AG_CHUNKS)
@@ -428,7 +427,7 @@
             dma((2,)), dma((SIB_SLOTS,)),
             pltpu.SemaphoreType.REGULAR,
         ],
-        compiler_params=pltpu.CompilerParams(collective_id=0, has_side_effects=True, vmem_limit_bytes=58 << 20),
+        compiler_params=pltpu.CompilerParams(collective_id=0, has_side_effects=True, vmem_limit_bytes=61 << 20),
     )(tokens, ids, gates, slot_ids, w_gate, w_up, w_down)
 
 

time: 258 us -> 252 us (0.977)
  Pallas kernels: 257 us -> 251 us
    pallas_call x1, Pallas kernels: 257 us -> 251 us  [group_layer(): pl.pallas_call(functools.partial(moe_kernel, (n, cap, spad, n_w)), out_sh...]
where the time goes in v8:
time: 252 us
  Pallas kernels  251 us (100%)
    pallas_call x1, Pallas kernels, group_layer(): pl.pallas_call(functools.partial(moe_kernel, (n, cap, spad, n_w)), out_sh...  251 us

profile of v8, /device:TPU:21, one launch (start us, length us, event | category | flops | bytes accessed | tf_op | source)
XLA Modules:
  0.0 252.2 jit_solution(16257653895579251750)
XLA Ops:
  0.0 251.2 %shard_map.73 = bf16[256,2048]{1,0:T(8,128)(2,1)S(1)} custom-call(bf16[256,2048]{1,0:T(8,128)(2,1)} %tok_in.1, s32[8,256]{1,0:T(8,128)} %bitcast.3, f32[8,256]{1,0:T(8,128)} %bitcast.4, s32[8,256]{1,0:T(8,128)} %bitcast.5, bf16[4,2048,1024]{2,1,0:T(8,128)(2,1)} %wg.1, bf16[4,2048,1024]{2,1,0:T(8,128)(2,1)} %wu.1, bf16[4,1024,2048]{2,1,0:T(8,128)(2,1)} %wd.1), custom_call_target="tpu_custom_call" | custom-call | tf_op jit(solution)/shard_map/pallas_call | solution.py:403
  251.2 1.0 copy.9

commit v9 on v6

--- a/solution.py
+++ b/solution.py
@@ -280,8 +280,9 @@
                     load_down(idx + n_w + k - up_loads, slot + k, begin)
             if events:
                 every = max(n_exp * n_f // max(n_events - 2, 1), 1)
-
-                @pl.when((step % every == every - 1) & (step // every < n_events - 2))
+                early = every * 3 // 4 - 1 if every > 1 else 0
+
+                @pl.when((step % every == early) & (step // every < n_events - 2))
                 def _():
                     second_half_event(step // every)
             return carry
@@ -381,7 +382,7 @@
                 close(d - 1)
             if events:
                 for k in range(2):
-                    @pl.when(d == (k + 1) * n_d // 2 - 1)
+                    @pl.when(d == max((k + 1) * n_d // 2 - 2, k))
                     def _():
                         second_half_event(n_events - 2 + k)
             return carry

time: 252 us -> 253 us (level)
  no operation moved by 1% of the time
where the time goes in v9:
time: 253 us
  Pallas kernels  252 us (100%)
    pallas_call x1, Pallas kernels, group_layer(): pl.pallas_call(functools.partial(moe_kernel, (n, cap, spad, n_w)), out_sh...  252 us

profile of v9, /device:TPU:21, one launch (start us, length us, event | category | flops | bytes accessed | tf_op | source)
XLA Modules:
  0.0 252.6 jit_solution(1836063303187179596)
XLA Ops:
  0.0 251.6 %shard_map.73 = bf16[256,2048]{1,0:T(8,128)(2,1)S(1)} custom-call(bf16[256,2048]{1,0:T(8,128)(2,1)} %tok_in.1, s32[8,256]{1,0:T(8,128)} %bitcast.3, f32[8,256]{1,0:T(8,128)} %bitcast.4, s32[8,256]{1,0:T(8,128)} %bitcast.5, bf16[4,2048,1024]{2,1,0:T(8,128)(2,1)} %wg.1, bf16[4,2048,1024]{2,1,0:T(8,128)(2,1)} %wu.1, bf16[4,1024,2048]{2,1,0:T(8,128)(2,1)} %wd.1), custom_call_target="tpu_custom_call" | custom-call | tf_op jit(solution)/shard_map/pallas_call | solution.py:478
  251.6 1.0 copy.9
